TPU v7x, 256 devices: a whole 4x4x8 slice. The times are simulated.
256 devices in a mesh: dp: 8 (over y, core), head: 2 (over z_lo), kv: 16 (over z_hi, x).
Axes of the slice: x: 4, y: 4, z: 8 (z_hi: 4, z_lo: 2; z = z_hi * 2 + z_lo), core: 2. Of those that a mesh axis runs over, the one named last changes fastest.
Arguments:
- teacher_query: bfloat16 [8, 4096, 3584], P('dp', 'kv', 'head'), may hold values from -96 to 96
- teacher_key: bfloat16 [8, 4096, 512], P('dp', 'kv', 'head'), may hold values from -8 to 8
- student_query: bfloat16 [8, 4096, 1792], P('dp', 'kv', 'head'), may hold values from -96 to 96
- student_key: bfloat16 [8, 4096, 256], P('dp', 'kv', 'head'), may hold values from -8 to 8
- pair_table: int32 [14, 2], replicated, may hold values from 0 to 27, as said below
Outputs:
- kl: float32 [8, 14, 4096], P('dp', 'head', 'kv')
- head_loss: float32 [14], P('head')
Inputs may be any that keep to these rules, and one draw needn't show every extreme that they name: `pair_table`: each of the 28 teacher heads appears exactly once in the table.
All inputs are finite; a program needn't handle non-finite values.
Results may differ from a plain program's by a relative error of at most 0.0003.
Values may be sent and summed in bfloat16 or wider, within the bound.
A program may use at most 64 MiB of HBM per device.

v0:
```python
import math

import jax
import jax.numpy as jnp
from jax import lax
from jax.sharding import Mesh
from jax.sharding import PartitionSpec as P

HT = 28
KVT = 4
DH = 128
HS = 14
KVS = 2
KV = ("kv_0", "kv_1")
DP = ("dp_0", "dp_1")
DP_KV = ("dp_0", "dp_1", "kv_0", "kv_1")


masked_value = -1e30


def from_everyone(shard, axis):
    count = lax.axis_size(axis)
    return lax.all_to_all(
        jnp.broadcast_to(shard[None], (count, *shard.shape)), axis, 0, 0, tiled=True
    )


def joined_along(blocks, dim):
    dims = list(blocks.shape[1:])
    dims[dim] *= blocks.shape[0]
    return jnp.moveaxis(blocks, 0, dim).reshape(dims)


def gathered_copies(shard, axis, dim):
    blocks = from_everyone(shard, axis)
    return joined_along(blocks, dim)


def one_axis_at_a_time(shard, axes):
    for axis in axes:
        shard = lax.psum(shard, axis)
    return shard


def running_softmax(running_max, running_total, logits, causal_mask):
    filled = jnp.where(causal_mask, logits, masked_value)
    new_max = jnp.maximum(running_max, jnp.max(filled, axis=-1))
    rescale = jnp.exp(running_max - new_max)
    weights = jnp.where(causal_mask, jnp.exp(filled - new_max[..., None]), 0.0)
    return (new_max, running_total * rescale + jnp.sum(weights, axis=-1), rescale, weights)


def make_fold(teacher_heads, teacher_select, student_heads, student_select, repeat, query_pos):
    seq_dev, row_count, pair_count, head_dim = teacher_heads.shape
    student_count = student_heads.shape[2]
    scale = 1.0 / math.sqrt(head_dim)
    last_query = query_pos[row_count - 1]

    def fold_step(carry, pieces, start):
        teacher_keys, student_keys = pieces
        key_count = teacher_keys.shape[1]
        block_size = math.gcd(key_count, 512)
        block_total = key_count // block_size
        visible = jnp.clip(last_query // block_size + 1, 0, block_total)

        def one_block(block_index, state):
            t_max, t_total, t_cross, s_max, s_total = state
            offset = block_index * block_size
            t_block = lax.dynamic_slice_in_dim(teacher_keys, offset, block_size, 1).reshape(
                seq_dev, block_size, -1, head_dim
            )
            s_block = lax.dynamic_slice_in_dim(student_keys, offset, block_size, 1).reshape(
                seq_dev, block_size, -1, head_dim
            )
            t_keys = jnp.take(t_block, teacher_select, axis=2)
            s_keys = jnp.take(s_block, student_select, axis=2)
            t_logits = (
                jnp.einsum(
                    "bqpd,bkpd->bpqk", teacher_heads, t_keys, preferred_element_type=jnp.float32
                )
                * scale
            )
            s_logits = (
                jnp.einsum(
                    "bqsd,bksd->bsqk", student_heads, s_keys, preferred_element_type=jnp.float32
                )
                * scale
            )
            key_pos = offset + jnp.arange(block_size, dtype=jnp.int32)
            causal_mask = key_pos[None, :] <= query_pos[:, None]
            t_max, t_total, t_rescale, t_weights = running_softmax(
                t_max, t_total, t_logits, causal_mask
            )
            s_max, s_total, s_rescale, s_weights = running_softmax(
                s_max, s_total, s_logits, causal_mask
            )
            split_logits = t_logits.reshape(seq_dev, student_count, repeat, row_count, block_size)
            gap = (split_logits - s_logits[:, :, None]).reshape(
                seq_dev, pair_count, row_count, block_size
            )
            t_cross = t_cross * t_rescale + jnp.sum(t_weights * gap, axis=-1)
            return (t_max, t_total, t_cross, s_max, s_total)

        return lax.fori_loop(0, visible, one_block, carry)

    pair_shape = (seq_dev, pair_count, row_count)
    student_shape = (seq_dev, student_count, row_count)
    initial = (
        jnp.full(pair_shape, masked_value, jnp.float32),
        jnp.zeros(pair_shape, jnp.float32),
        jnp.zeros(pair_shape, jnp.float32),
        jnp.full(student_shape, masked_value, jnp.float32),
        jnp.zeros(student_shape, jnp.float32),
    )
    return (fold_step, initial)


def finish_pairs(state, repeat):
    t_max, t_total, t_cross, s_max, s_total = state
    seq_dev, pair_count, row_count = t_max.shape
    student_count = s_max.shape[1]
    t_lse = t_max + jnp.log(t_total)
    s_lse = s_max + jnp.log(s_total)
    s_paired = jnp.broadcast_to(
        s_lse[:, :, None], (seq_dev, student_count, repeat, row_count)
    ).reshape(seq_dev, pair_count, row_count)
    return t_cross / t_total - t_lse + s_paired


def per_device(teacher_query, teacher_key, student_query, student_key, pair_table):
    seq_dev, row_count, teacher_width = teacher_query.shape
    n_head = lax.axis_size("head")
    n_kv = lax.axis_size(KV)
    n_data = lax.axis_size(DP)
    head_index = lax.axis_index("head")
    kv_index = lax.axis_index(KV)
    group_teacher = HT // KVT
    group_student = HS // KVS
    local_student = HS // n_head
    local_student_kv = KVS // n_head
    query_pos = kv_index * row_count + jnp.arange(row_count, dtype=jnp.int32)
    all_tq, all_tk = (
        gathered_copies(teacher_query, "head", 2),
        gathered_copies(teacher_key, "head", 2),
    )
    my_pairs = lax.dynamic_slice_in_dim(
        pair_table, head_index * local_student, local_student, 0
    ).reshape(-1)
    teacher_heads = jnp.take(all_tq.reshape(seq_dev, row_count, HT, DH), my_pairs, axis=2)
    teacher_select = my_pairs // group_teacher
    student_heads = student_query.reshape(seq_dev, row_count, local_student, DH)
    student_ids = head_index * local_student + jnp.arange(local_student, dtype=jnp.int32)
    student_select = student_ids // group_student - head_index * local_student_kv
    fold_step, initial = make_fold(
        teacher_heads, teacher_select, student_heads, student_select, 2, query_pos
    )
    state = fold_step(
        initial,
        (
            lax.all_gather(all_tk, KV, axis=1, tiled=True),
            lax.all_gather(student_key, KV, axis=1, tiled=True),
        ),
        jnp.int32(0),
    )
    pair_kl = finish_pairs(state, 2)
    kl_local = jnp.sum(pair_kl.reshape(seq_dev, local_student, 2, row_count), axis=2)
    head_sums = jnp.sum(kl_local, axis=(0, 2))
    total = one_axis_at_a_time(head_sums, DP_KV)
    head_loss = total / (seq_dev * n_data * row_count * n_kv)
    return (kl_local, head_loss)


def solution(mesh):
    split = Mesh(
        mesh.devices.reshape(4, 2, mesh.shape["head"], 4, 4),
        ("dp_0", "dp_1", "head", "kv_0", "kv_1"),
    )
    in_specs = (P(DP, KV, "head"), P(DP, KV, "head"), P(DP, KV, "head"), P(DP, KV, "head"), P())
    out_specs = (P(DP, "head", KV), P("head"))
    return jax.shard_map(
        per_device, mesh=split, in_specs=in_specs, out_specs=out_specs, check_vma=False
    )
```

profile of v0, /device:TPU:1, one launch (start us, length us, event | category | flops | bytes accessed | tf_op | source)
XLA Modules:
  0.0 261.9 jit_solution(12517146968400585087)
XLA Ops:
  7.2 0.7 all-gather.5.cloned.1.call-update
  8.0 1.0 copy.25
  9.0 8.1 %all_to_all.10 = bf16[2,1,256,256]{2,3,1,0:T(8,128)(2,1)} all-to-all(bf16[2,1,256,256]{2,3,1,0:T(8,128)(2,1)S(1)} %broadcast_in_dim.98), channel_id=1, replica_groups=mesh['dp_0'=4,'dp_1'=2,'head'=2,'kv_0'=4,'kv_1'=4] {'head'}, dimensions={0} | all-to-all | bytes 524288 | tf_op jit(solution)/shard_map/all_to_all | solution.py:24
  17.1 1.5 copy.26
  18.6 1.4 broadcast_in_dim.101
  20.0 3.7 %all-to-all-start.1 = ((bf16[2,1,256,1792]{2,3,1,0:T(8,128)(2,1)}), bf16[2,1,256,1792]{2,3,1,0:T(8,128)(2,1)S(1)}, u32[]{:S(2)}, u32[]{:S(2)}) async-start(bf16[2,1,256,1792]{2,3,1,0:T(8,128)(2,1)} %broadcast_in_dim.101), calls=%async_computation.1 | async-start | bytes 3670016 | tf_op jit(solution)/shard_map/all_to_all | solution.py:24
  27.5 1.0 copy.31
  28.5 16.5 %all-to-all-done.1 = bf16[2,1,256,1792]{2,3,1,0:T(8,128)(2,1)S(1)} async-done(((bf16[2,1,256,1792]{2,3,1,0:T(8,128)(2,1)}), bf16[2,1,256,1792]{2,3,1,0:T(8,128)(2,1)S(1)}, u32[]{:S(2)}, u32[]{:S(2)}) %all-to-all-start.1) | async-done | bytes 1835040 | tf_op jit(solution)/shard_map/all_to_all | solution.py:24
  45.0 2.6 copy.29
  47.6 2.2 gather_fusion.1
  50.0 16.4 %all-gather.5.cloned.1.call-done = bf16[1,4096,128]{2,1,0:T(8,128)(2,1)} async-done(((bf16[1,256,128]{2,1,0:T(8,128)(2,1)}), bf16[1,4096,128]{2,1,0:T(8,128)(2,1)}) %all-gather.5.cloned.1.call-update) | async-done | bytes 1048592 | tf_op jit(solution)/shard_map/all_gather | solution.py:162
  66.4 82.6 %all-gather.3.cloned.1.call-done = bf16[1,4096,512]{1,2,0:T(8,128)(2,1)} async-done(((bf16[1,256,512]{1,2,0:T(8,128)(2,1)}), bf16[1,4096,512]{1,2,0:T(8,128)(2,1)}) %all-gather.3.cloned.1.call-update) | async-done | bytes 4194320 | tf_op jit(solution)/shard_map/all_gather | solution.py:161
  149.0 9.1 %while.19 = (s32[]{:T(128)}, f32[1,14,256]{2,1,0:T(8,128)S(1)}, f32[1,14,256]{2,1,0:T(8,128)S(1)}, f32[1,14,256]{2,1,0:T(8,128)S(1)}, f32[1,7,256]{2,1,0:T(8,128...) while((s32[]{:T(128)}, f32[1,14,256]{2,1,0:T(8,128)S(1)}, ...), condition=%wide.region_6.7_spmd.clone, body=%wide.region_0.6_spmd.clone.sunk | while | flops 732774400 | bytes 37899856 | solution.py:105
  149.0 1.1 constant_dynamic-slice_fusion.3
  150.4 0.9 gather_fusion
  151.5 1.4 fusion.28
  152.9 0.9 dynamic-slice_bitcast_fusion.2
  153.9 0.8 select_reduce_fusion.4
  154.7 2.6 fusion.29
  157.3 0.8 select_reduce_fusion.5
  158.5 6.0 %psum.28 = f32[7]{0:T(128)S(1)} all-reduce(f32[7]{0:T(128)S(1)} %reduce_sum.64), channel_id=1, replica_groups=mesh['dp_0'=4,'dp_1'=2,'head'=2,'kv_0'=4,'kv_1'=4] {'dp_0'}, use_global_device_ids=true, to_apply=%region_10.11 | all-reduce | flops 7 | bytes 56 | tf_op jit(solution)/shard_map/psum | solution.py:42
  164.5 7.7 %psum.29 = f32[7]{0:T(128)S(1)} all-reduce(f32[7]{0:T(128)S(1)} %psum.28), channel_id=1, replica_groups=mesh['dp_0'=4,'dp_1'=2,'head'=2,'kv_0'=4,'kv_1'=4] {'dp_1'}, use_global_device_ids=true, to_apply=%region_11.12 | all-reduce | flops 7 | bytes 56 | tf_op jit(solution)/shard_map/psum | solution.py:42
  172.2 63.0 %psum.30 = f32[7]{0:T(128)S(1)} all-reduce(f32[7]{0:T(128)S(1)} %psum.29), channel_id=1, replica_groups=mesh['dp_0'=4,'dp_1'=2,'head'=2,'kv_0'=4,'kv_1'=4] {'kv_0'}, use_global_device_ids=true, to_apply=%region_12.13 | all-reduce | flops 7 | bytes 56 | tf_op jit(solution)/shard_map/psum | solution.py:42
  235.8 18.8 %psum.31 = f32[7]{0:T(128)S(1)} all-reduce(f32[7]{0:T(128)S(1)} %psum.30), channel_id=1, replica_groups=mesh['dp_0'=4,'dp_1'=2,'head'=2,'kv_0'=4,'kv_1'=4] {'kv_1'}, use_global_device_ids=true, to_apply=%region_13.14 | all-reduce | flops 7 | bytes 56 | tf_op jit(solution)/shard_map/psum | solution.py:42
  (51 shorter events, 3.5 us)
Async XLA Ops:
  7.2 19.1 %copy-start = (s32[14,2]{0,1:T(2,128)S(1)}, s32[14,2]{0,1:T(2,128)}, u32[]{:S(2)}) copy-start(s32[14,2]{0,1:T(2,128)} %param.11) | copy-start | bytes 340
  7.2 59.2 %all-gather.5.cloned.1.call-start = ((), (), s32[]{:S(2)}) async-start(), calls=%async_computation.3 | async-start | bytes 1114112 | tf_op jit(solution)/shard_map/all_gather | solution.py:162
  7.9 141.1 %all-gather.3.cloned.1.call-start = ((), (), s32[]{:S(2)}) async-start(), calls=%async_computation.2 | async-start | bytes 4456448 | tf_op jit(solution)/shard_map/all_gather | solution.py:161
  18.6 8.7 %copy-start.1 = (bf16[1,256,896]{2,1,0:T(8,128)(2,1)S(1)}, bf16[1,256,896]{2,1,0:T(8,128)(2,1)}, u32[]{:S(2)}) copy-start(bf16[1,256,896]{2,1,0:T(8,128)(2,1)} %param.9) | copy-start | bytes 1376260
  20.0 25.0 %all-to-all-start.1 = ((bf16[2,1,256,1792]{2,3,1,0:T(8,128)(2,1)}), bf16[2,1,256,1792]{2,3,1,0:T(8,128)(2,1)S(1)}, u32[]{:S(2)}, u32[]{:S(2)}) async-start(bf16[2,1,256,1792]{2,3,1,0:T(8,128)(2,1)} %broadcast_in_dim.101), calls=%async_computation.1 | async-start | bytes 3670016 | tf_op jit(solution)/shard_map/all_to_all | solution.py:24
  151.5 2.4 copy-start.2
Sparse Core Ops, SparseCore 0:
  10.4 55.9 all-gather.4
  68.8 80.1 all-gather.2
where the time goes:
time: 264 us; the launch traced here: 262 us
  waiting for transfers between devices  116 us (44%)
  blocking collectives  104 us (39%)
  between operations  16.8 us (6%)
  local copies, waits for them, and re-layouts  14.7 us (6%)
  other arithmetic  4.56 us (2%)
  starting transfers between devices  3.79 us (1%)
    psum x4, blocking collectives, one_axis_at_a_time(): shard = lax.psum(shard, axis)  95.4 us
    all_gather x1, waiting for transfers between devices, per_device(): lax.all_gather(all_tk, KV, axis=1, tiled=True)  82.6 us
    all_to_all x1, waiting for transfers between devices, from_everyone(): lax.all_to_all(jnp.broadcast_to(shard[None], (count, *shard.shape)), axis...  16.5 us
    all_gather x1, waiting for transfers between devices, per_device(): lax.all_gather(student_key, KV, axis=1, tiled=True)  16.4 us
    all_to_all x1, blocking collectives, from_everyone(): lax.all_to_all(jnp.broadcast_to(shard[None], (count, *shard.shape)), axis...  8.11 us
  transfers between devices with their start and end apart: 3, of which 3 were waited for; matrix products, arithmetic and copies ran while one was open for 4% of the time, Pallas kernels for 0%

commit v1 on v0

v1 whole, which is shorter than its diff:
```python
import math

import jax
import jax.numpy as jnp
from jax import lax
from jax.experimental import pallas as pl
from jax.experimental.pallas import tpu as pltpu
from jax.sharding import PartitionSpec as P

HT = 28
HS = 14
DH = 128
GROUP = 7
NX = 4
NZ = 4
N_KV = NX * NZ
N_DP = 8
ROWS = 256
CHUNK = 128
HALF = CHUNK // 2
TILE = NX * CHUNK
T_LOCAL = 14
S_LOCAL = 7
SCALE = 1.0 / math.sqrt(DH)
LOG2E = math.log2(math.e)
LN2 = math.log(2.0)
NEG = -1e30
MESH = pl.DeviceIdType.MESH
NT = (((1,), (1,)), ((), ()))


def split_scaled(q):
    scaled = q.astype(jnp.float32) * (SCALE * LOG2E)
    hi = scaled.astype(jnp.bfloat16)
    lo = (scaled - hi.astype(jnp.float32)).astype(jnp.bfloat16)
    return jnp.concatenate([hi, lo], axis=1)


def kernel(
    table,
    tq,
    tk_in,
    sq_in,
    sk_in,
    kl_out,
    loss_out,
    keys,
    sq,
    qy,
    qg,
    qs,
    t_state,
    s_state,
    y_a,
    g_a,
    y_b,
    g_b,
    y_s,
    bias,
    contrib,
    kl_other,
    sums_plane,
    sums_dp,
    group_table,
    student_table,
    local_sem,
    swap_send,
    swap_recv,
    z_send,
    z_recv,
    relay_send,
    x1_send,
    x1_recv,
    x2_send,
    x2_recv,
    kl_sem,
    plane_send,
    plane_recv,
    dp_send,
    dp_recv,
):
    dp = lax.axis_index("dp")
    head = lax.axis_index("head")
    kv = lax.axis_index("kv")
    row = kv // NX
    col = kv % NX
    right = row * NX + (col + 1) % NX
    left = row * NX + (col + NX - 1) % NX

    def device(d, h, k):
        return (d, h, k)

    def remote(src, dst, send_sem, recv_sem, dev):
        return pltpu.make_async_remote_copy(
            src_ref=src,
            dst_ref=dst,
            send_sem=send_sem,
            recv_sem=recv_sem,
            device_id=dev,
            device_id_type=MESH,
        )

    s_lane = pl.multiple_of(256 + head * 128, 128)
    fill_t = pltpu.make_async_copy(tk_in.at[0], keys.at[kv, :, pl.ds(0, 256)], local_sem.at[0])
    fill_s = pltpu.make_async_copy(sk_in.at[0], keys.at[kv, :, pl.ds(s_lane, 128)], local_sem.at[1])
    fill_q = pltpu.make_async_copy(sq_in.at[0], sq.at[head], local_sem.at[2])
    fill_s.start()
    fill_t.start()
    fill_q.start()

    barrier = pltpu.get_barrier_semaphore()

    def greet_plane(i, _):
        peer = (head * N_KV + kv + i) % (2 * N_KV)
        pl.semaphore_signal(
            barrier,
            inc=1,
            device_id=device(dp, peer // N_KV, peer % N_KV),
            device_id_type=MESH,
        )
        return 0

    lax.fori_loop(1, 2 * N_KV, greet_plane, 0)

    def greet_dp(i, _):
        pl.semaphore_signal(
            barrier, inc=1, device_id=device((dp + i) % N_DP, head, kv), device_id_type=MESH
        )
        return 0

    lax.fori_loop(1, N_DP, greet_dp, 0)
    pl.semaphore_wait(barrier, 2 * N_KV - 1 + N_DP - 1)

    partner = device(dp, 1 - head, kv)
    fill_s.wait()
    swap_s = remote(
        keys.at[kv, :, pl.ds(s_lane, 128)],
        keys.at[kv, :, pl.ds(s_lane, 128)],
        swap_send.at[0],
        swap_recv.at[0],
        partner,
    )
    swap_s.start()
    fill_q.wait()
    swap_q = remote(sq.at[head], sq.at[head], swap_send.at[1], swap_recv.at[1], partner)

    bias_col = col * ROWS + lax.broadcasted_iota(jnp.int32, (TILE, ROWS), 1)
    bias_pos = lax.broadcasted_iota(jnp.int32, (TILE, ROWS), 0)
    bias_key = bias_pos + (bias_pos // CHUNK) * (ROWS - CHUNK)
    for c in range(2):
        bias[c] = jnp.where(bias_key + c * CHUNK <= bias_col, 0.0, NEG)

    def columns(h):
        return pl.ds(pl.multiple_of(h * DH, DH), DH)

    fill_t.wait()
    other_lane = pl.multiple_of(384 - head * 128, 128)
    landed_s = remote(
        keys.at[kv, :, pl.ds(other_lane, 128)],
        keys.at[kv, :, pl.ds(other_lane, 128)],
        swap_send.at[0],
        swap_recv.at[0],
        partner,
    )
    landed_s.wait_recv()

    def z_copy(slot_row, c, send_sem, target_row):
        block = keys.at[slot_row * NX + col, pl.ds(c * CHUNK, CHUNK)]
        return remote(
            block, block, send_sem, z_recv.at[slot_row, c], device(dp, head, target_row * NX + col)
        )

    def up(c):
        return z_copy(row, c, z_send.at[0, c], row + 1)

    def down(c):
        return z_copy(row, c, z_send.at[1, c], (row + NZ - 1) % NZ)

    has_up = row < NZ - 1
    has_down = row < 2

    def forward(slot_row, c):
        return z_copy(slot_row, c, relay_send.at[c], jnp.where(row == 0, NZ - 1, row + 1))

    def x1(slot_row, c, side, target):
        block = keys.at[slot_row * NX + col, pl.ds(c * CHUNK, CHUNK)]
        return remote(
            block,
            block,
            x1_send.at[slot_row, c, side],
            x1_recv.at[slot_row, c, side],
            device(dp, head, target),
        )

    def x1_arrival(slot_row, c, side, source_col):
        block = keys.at[slot_row * NX + source_col, pl.ds(c * CHUNK, CHUNK)]
        return remote(
            block,
            block,
            x1_send.at[slot_row, c, side],
            x1_recv.at[slot_row, c, side],
            device(dp, head, right),
        )

    def x2(slot_row, c, side, source_col, target):
        block = keys.at[
            slot_row * NX + source_col, pl.ds(c * CHUNK + side * HALF, HALF)
        ]
        return remote(
            block,
            block,
            x2_send.at[slot_row, c, side],
            x2_recv.at[slot_row, c, side],
            device(dp, head, target),
        )

    left_col = (col + NX - 1) % NX
    right_col = (col + 1) % NX
    far_col = (col + 2) % NX

    def wave(w):
        early = w < 2
        last = row == NZ - 1
        k = w // 2
        r_last = jnp.where(w >= 6, 1, jnp.where(w % 2 == 0, 2, 0))
        c_last = jnp.where(w >= 6, w - 6, (w - 2) // 2)
        r = jnp.where(early, row, jnp.where(last, r_last, row - k))
        c = jnp.where(early, w, jnp.where(last, c_last, w % 2))
        return r, c

    def start_x1(r, c):
        x1(r, c, 0, right).start()
        x1(r, c, 1, left).start()

    def z_event(w):
        r, c = wave(w)
        z_copy(r, c, relay_send.at[c], row).wait_recv()
        start_x1(r, c)

        @pl.when((row == 1) & (r == 0))
        def _():
            forward(0, c).start()

    def x_event(w):
        r, c = wave(w)
        x1_arrival(r, c, 0, left_col).wait_recv()
        x2(r, c, 0, left_col, right).start()
        x1_arrival(r, c, 1, right_col).wait_recv()
        x2(r, c, 1, right_col, left).start()

    def d_event(w):
        r, c = wave(w)
        x2(r, c, 0, far_col, right).wait_recv()
        x2(r, c, 1, far_col, right).wait_recv()

    for c in range(2):
        start_x1(row, c)

        @pl.when(has_up)
        def _():
            up(c).start()

        @pl.when(has_down)
        def _():
            down(c).start()

    swap_q.start()

    def prepare(t, _):
        qy[t] = split_scaled(tq[0, :, columns(t)])
        t_state[t] = jnp.concatenate(
            [jnp.full((8, ROWS), NEG, jnp.float32), jnp.zeros((16, ROWS), jnp.float32)], axis=0
        )
        return 0

    lax.fori_loop(0, T_LOCAL, prepare, 0)

    def prepare_student(t, _):
        qs[t] = split_scaled(sq[head, :, columns(t)])
        s_state[t] = jnp.concatenate(
            [jnp.full((8, ROWS), NEG, jnp.float32), jnp.zeros((8, ROWS), jnp.float32)], axis=0
        )
        return 0

    lax.fori_loop(0, S_LOCAL, prepare_student, 0)

    waves = 2 * (row + 1)
    x_event(0)
    x_event(1)

    @pl.when(row == 0)
    def _():
        for c in range(2):
            z_copy(1, c, relay_send.at[c], row).wait_recv()
            forward(1, c).start()

    @pl.when(row > 0)
    def _():
        z_event(2)
        z_event(3)

    def student_of(t):
        found = jnp.int32(0)
        for e in range(HT):
            found = jnp.where(table[e] == head * T_LOCAL + t, e // 2, found)
        return found

    students = [student_of(t) for t in range(T_LOCAL)]
    for t in range(T_LOCAL):
        student_table[t] = students[t]
        group_table[t] = jnp.where(students[t] >= GROUP, 1, 0)

    remote(sq.at[1 - head], sq.at[1 - head], swap_send.at[1], swap_recv.at[1], partner).wait_recv()

    def prepare_gap(t, _):
        s = student_table[t]
        student_q = sq[0, :, 0:DH]
        for e in range(1, HS):
            candidate = sq[e // GROUP, :, (e % GROUP) * DH : (e % GROUP + 1) * DH]
            student_q = jnp.where(s == e, candidate, student_q)
        qg[t] = jnp.concatenate([tq[0, :, columns(t)], -student_q], axis=1)
        return 0

    lax.fori_loop(0, T_LOCAL, prepare_gap, 0)

    def compute(r, c, masked):
        def tile(lanes):
            return keys[pl.ds(r * NX, NX), pl.ds(c * CHUNK, CHUNK), lanes].reshape(TILE, 128)

        def product(lhs, rhs):
            return lax.dot_general(lhs, rhs, NT, preferred_element_type=jnp.float32)

        def teacher_products(t, group, lane, y_buf, g_buf):
            k = tile(pl.ds(lane, 128))
            ks = jnp.where(group == 0, tile(pl.ds(256, 128)), tile(pl.ds(384, 128)))
            y_buf[...] = product(jnp.concatenate([k, k], axis=1), qy[t])
            g_buf[...] = product(jnp.concatenate([k, ks], axis=1), qg[t])

        def student_products(t):
            k = tile(pl.ds(s_lane, 128))
            y_s[...] = product(jnp.concatenate([k, k], axis=1), qs[t])

        def weights(y_buf, running_max):
            y = y_buf[...]
            if masked:
                y = y + bias[c]
            y = y.reshape(TILE // 8, 8, ROWS)
            new_max = jnp.maximum(running_max, jnp.max(y, axis=0))
            return new_max, jnp.exp2(running_max - new_max), jnp.exp2(y - new_max[None])

        def teacher_update(t, y_buf, g_buf):
            new_max, rescale, p = weights(y_buf, t_state[t, 0:8])
            t_state[t, 0:8] = new_max
            t_state[t, 8:16] = t_state[t, 8:16] * rescale + jnp.sum(p, axis=0)
            t_state[t, 16:24] = t_state[t, 16:24] * rescale + jnp.sum(
                p * g_buf[...].reshape(p.shape), axis=0
            )

        def student_update(t):
            new_max, rescale, p = weights(y_s, s_state[t, 0:8])
            s_state[t, 0:8] = new_max
            s_state[t, 8:16] = s_state[t, 8:16] * rescale + jnp.sum(p, axis=0)

        teacher_products(0, group_table[0], 0, y_a, g_a)

        def step(j, _):
            following = jnp.minimum(j + 1, GROUP - 1)
            teacher_products(GROUP + j, group_table[GROUP + j], 128, y_b, g_b)
            student_products(j)
            teacher_update(j, y_a, g_a)
            teacher_products(following, group_table[following], 0, y_a, g_a)
            teacher_update(GROUP + j, y_b, g_b)
            student_update(j)
            return 0

        lax.fori_loop(0, GROUP, step, 0)

    for w in range(2):

        @pl.when(w + 4 < waves)
        def _():
            z_event(w + 4)

        @pl.when(w + 2 < waves)
        def _():
            x_event(w + 2)

        d_event(w)
        compute(row, w, True)

    def later(w, _):
        @pl.when(w + 4 < waves)
        def _():
            z_event(w + 4)

        @pl.when(w + 2 < waves)
        def _():
            x_event(w + 2)

        d_event(w)
        r, c = wave(w)
        compute(r, c, False)
        return 0

    lax.fori_loop(2, waves, later, 0)

    lane_row = lax.broadcasted_iota(jnp.int32, (8, ROWS), 0)
    parts = [jnp.zeros((8, ROWS), jnp.float32), jnp.zeros((8, ROWS), jnp.float32)]
    for t in range(T_LOCAL):
        m = t_state[t, 0:8]
        top = jnp.max(m, axis=0, keepdims=True)
        w = jnp.exp2(m - top)
        total = jnp.sum(t_state[t, 8:16] * w, axis=0, keepdims=True)
        cross = jnp.sum(t_state[t, 16:24] * w, axis=0, keepdims=True)
        value = cross / total * SCALE - (top + jnp.log2(total)) * LN2
        for g in range(2):
            parts[g] = parts[g] + jnp.where(lane_row == students[t] - g * GROUP, value, 0.0) * jnp.where(
                (students[t] >= GROUP) == (g == 1), 1.0, 0.0
            )
    home = jnp.zeros((8, ROWS), jnp.float32)
    for t in range(S_LOCAL):
        m = s_state[t, 0:8]
        top = jnp.max(m, axis=0, keepdims=True)
        total = jnp.sum(s_state[t, 8:16] * jnp.exp2(m - top), axis=0, keepdims=True)
        home = home + jnp.where(lane_row == t, (top + jnp.log2(total)) * (2.0 * LN2), 0.0)
    for g in range(2):
        contrib[g] = parts[g] + jnp.where(head == g, home, 0.0)
    kl_copy = remote(contrib.at[1 - head], kl_other, kl_sem.at[0], kl_sem.at[1], partner)
    kl_copy.start()

    me = head * N_KV + kv
    for g in range(2):
        block = jnp.sum(contrib[g], axis=1, keepdims=True)
        sums_plane[2 * N_KV + g] = jnp.broadcast_to(block, (8, 128))

    def plane_copy(i):
        peer = (me + i) % (2 * N_KV)
        return remote(
            sums_plane.at[2 * N_KV + peer // N_KV],
            sums_plane.at[me],
            plane_send.at[i],
            plane_recv.at[me],
            device(dp, peer // N_KV, peer % N_KV),
        )

    def plane_start(i, _):
        plane_copy(i).start()
        return 0

    lax.fori_loop(1, 2 * N_KV, plane_start, 0)

    kl_copy.wait()
    kl_out[0] = (contrib[head] + kl_other[...])[0:S_LOCAL]

    def plane_wait(i, total):
        source = (me + i) % (2 * N_KV)
        remote(
            sums_plane.at[source],
            sums_plane.at[source],
            plane_send.at[i],
            plane_recv.at[source],
            partner,
        ).wait_recv()
        return total + sums_plane[source]

    plane_total = lax.fori_loop(1, 2 * N_KV, plane_wait, sums_plane[2 * N_KV + head])
    sums_dp[N_DP] = plane_total

    def dp_copy(i):
        return remote(
            sums_dp.at[N_DP],
            sums_dp.at[dp],
            dp_send.at[i],
            dp_recv.at[dp],
            device((dp + i) % N_DP, head, kv),
        )

    for i in range(1, N_DP):
        dp_copy(i).start()
    grand = plane_total
    for i in range(1, N_DP):
        source = (dp + i) % N_DP
        remote(
            sums_dp.at[source], sums_dp.at[source], dp_send.at[i], dp_recv.at[source], partner
        ).wait_recv()
        grand = grand + sums_dp[source]
    loss_out[...] = grand * (1.0 / (N_DP * N_KV * ROWS))

    swap_s.wait_send()
    swap_q.wait_send()
    for c in range(2):

        @pl.when(has_up)
        def _():
            up(c).wait_send()

        @pl.when(has_down)
        def _():
            down(c).wait_send()

        @pl.when(row == 0)
        def _():
            forward(1, c).wait_send()

        @pl.when(row == 1)
        def _():
            forward(0, c).wait_send()

    def drain(w, _):
        r, c = wave(w)
        x1(r, c, 0, right).wait_send()
        x1(r, c, 1, left).wait_send()
        x2(r, c, 0, left_col, right).wait_send()
        x2(r, c, 1, right_col, left).wait_send()
        return 0

    lax.fori_loop(0, waves, drain, 0)

    def plane_drain(i, _):
        plane_copy(i).wait_send()
        return 0

    lax.fori_loop(1, 2 * N_KV, plane_drain, 0)
    for i in range(1, N_DP):
        dp_copy(i).wait_send()


def per_device(teacher_query, teacher_key, student_query, student_key, pair_table):
    vmem = pl.BlockSpec(memory_space=pltpu.VMEM)
    anywhere = pl.BlockSpec(memory_space=pl.ANY)
    dma = pltpu.SemaphoreType.DMA
    f32, bf16 = jnp.float32, jnp.bfloat16
    kl, loss = pl.pallas_call(
        kernel,
        out_shape=(
            jax.ShapeDtypeStruct((1, S_LOCAL, ROWS), f32),
            jax.ShapeDtypeStruct((8, 128), f32),
        ),
        in_specs=[pl.BlockSpec(memory_space=pltpu.SMEM), vmem, anywhere, anywhere, anywhere],
        out_specs=(vmem, vmem),
        scratch_shapes=[
            pltpu.VMEM((N_KV, ROWS, 512), bf16),
            pltpu.VMEM((2, ROWS, S_LOCAL * DH), bf16),
            pltpu.VMEM((T_LOCAL, ROWS, 256), bf16),
            pltpu.VMEM((T_LOCAL, ROWS, 256), bf16),
            pltpu.VMEM((S_LOCAL, ROWS, 256), bf16),
            pltpu.VMEM((T_LOCAL, 24, ROWS), f32),
            pltpu.VMEM((S_LOCAL, 16, ROWS), f32),
            pltpu.VMEM((TILE, ROWS), f32),
            pltpu.VMEM((TILE, ROWS), f32),
            pltpu.VMEM((TILE, ROWS), f32),
            pltpu.VMEM((TILE, ROWS), f32),
            pltpu.VMEM((TILE, ROWS), f32),
            pltpu.VMEM((2, TILE, ROWS), f32),
            pltpu.VMEM((2, 8, ROWS), f32),
            pltpu.VMEM((8, ROWS), f32),
            pltpu.VMEM((2 * N_KV + 2, 8, 128), f32),
            pltpu.VMEM((N_DP + 1, 8, 128), f32),
            pltpu.SMEM((T_LOCAL,), jnp.int32),
            pltpu.SMEM((T_LOCAL,), jnp.int32),
            dma((3,)),
            dma((2,)),
            dma((2,)),
            dma((2, 2)),
            dma((NZ, 2)),
            dma((2,)),
            dma((NZ, 2, 2)),
            dma((NZ, 2, 2)),
            dma((NZ, 2, 2)),
            dma((NZ, 2, 2)),
            dma((2,)),
            dma((2 * N_KV,)),
            dma((2 * N_KV,)),
            dma((N_DP,)),
            dma((N_DP,)),
        ],
        compiler_params=pltpu.CompilerParams(
            collective_id=0, has_side_effects=True, vmem_limit_bytes=60 * 1024 * 1024
        ),
    )(pair_table.reshape(-1), teacher_query, teacher_key, student_query, student_key)
    return kl, loss[:S_LOCAL, 0]


def solution(mesh):
    spec = P("dp", "kv", "head")
    return jax.shard_map(
        per_device,
        mesh=mesh,
        in_specs=(spec, spec, spec, spec, P()),
        out_specs=(P("dp", "head", "kv"), P("head")),
        check_vma=False,
    )
```

time: 264 us -> 95.3 us (0.36)
  waiting for transfers between devices: 116 us -> 0 us
  blocking collectives: 104 us -> 0 us
  Pallas kernels: 0 us -> 91.1 us
  between operations: 16.8 us -> 0.65 us
  local copies, waits for them, and re-layouts: 14.7 us -> 3.3 us
  other arithmetic: 4.56 us -> 0 us
  starting transfers between devices: 3.79 us -> 0 us
    all_gather x2 -> x0, waiting for transfers between devices: 99 us -> none  [the longest x1 82.6 us: per_device(): lax.all_gather(all_tk, KV, axis=1, tiled=True)]
    psum x4 -> x0, blocking collectives: 95.4 us -> none  [one_axis_at_a_time(): shard = lax.psum(shard, axis)]
    pallas_call x0 -> x1, Pallas kernels: none -> 91.1 us  [per_device(): pl.pallas_call(kernel, out_shape=(jax.ShapeDtypeStruct((1, S_LOCAL, ROWS)...]
    all_to_all x1 -> x0, waiting for transfers between devices: 16.5 us -> none  [from_everyone(): lax.all_to_all(jnp.broadcast_to(shard[None], (count, *shard.shape)), axis...]
    all_to_all x1 -> x0, blocking collectives: 8.11 us -> none  [from_everyone(): lax.all_to_all(jnp.broadcast_to(shard[None], (count, *shard.shape)), axis...]
    broadcast_in_dim x9 -> x0, local copies, waits for them, and re-layouts: 3.89 us -> none  [the longest x4 3.86 us: from_everyone(): jnp.broadcast_to(shard[None], (count, *shard.shape))]
    all_to_all x1 -> x0, starting transfers between devices: 3.72 us -> none  [from_everyone(): lax.all_to_all(jnp.broadcast_to(shard[None], (count, *shard.shape)), axis...]
    reduce_sum x5 -> x0, other arithmetic: 3.62 us -> none  [the longest x1 2.58 us: one_block(): t_cross = t_cross * t_rescale + jnp.sum(t_weights * gap, axis=-1)]
  transfers between devices with their start and end apart: 3 -> 0, of which waited for: 3 -> 0; matrix products, arithmetic and copies ran while one was open for 4% -> 0% of each run, Pallas kernels for 0% -> 0%
where the time goes in v1:
time: 95.3 us; the launch traced here: 95.1 us
  Pallas kernels  91.1 us (96%)
  local copies, waits for them, and re-layouts  3.3 us (3%)
    pallas_call x1, Pallas kernels, per_device(): pl.pallas_call(kernel, out_shape=(jax.ShapeDtypeStruct((1, S_LOCAL, ROWS)...  91.1 us
    unnamed x4, local copies, waits for them, and re-layouts  2.07 us

profile of v1, /device:TPU:1, one launch (start us, length us, event | category | flops | bytes accessed | tf_op | source)
XLA Modules:
  0.0 95.1 jit_solution(14296453212234694091)
XLA Ops:
  0.6 0.8 copy.9
  1.4 0.6 reshape.7.table
  2.0 91.1 %shard_map.68 = (f32[1,7,256]{2,1,0:T(8,128)}, f32[8,128]{1,0:T(8,128)}) custom-call(s32[28]{0:T(128)} %reshape.7.table, bf16[1,256,1792]{2,1,0:T(8,128)(2,1)} %tq.1, bf16[1,256,256]{2,1,0:T(8,128)(2,1)} %tk_in.1, bf16[1,256,896]{2,1,0:T(8,128)(2,1)} %sq_in.1, bf16[1,256,128]{2,1,0:T(8,128)(2,1)} %sk_in.1), custom_call_target="tpu_custom_call" | custom-call | tf_op jit(solution)/shard_map/pallas_call | solution.py:533
  93.2 0.0 copy-start
  93.2 1.3 %copy.10 = f32[1,7,256]{2,0,1:T(1,128)} copy(f32[1,7,256]{2,1,0:T(8,128)} %get-tuple-element.8) | data formatting | bytes 14336
  94.5 0.0 copy-done
  94.5 0.6 slice_reduce_fusion
Async XLA Ops:
  93.2 1.3 %copy-start = (f32[8,128]{1,0:T(8,128)S(1)}, f32[8,128]{1,0:T(8,128)}, u32[]{:S(2)}) copy-start(f32[8,128]{1,0:T(8,128)} %get-tuple-element.5) | copy-start | bytes 12292

commit v2 on v1

--- a/solution.py
+++ b/solution.py
@@ -1,3 +1,4 @@
+import functools
 import math
 
 import jax
@@ -18,7 +19,9 @@
 ROWS = 256
 CHUNK = 128
 HALF = CHUNK // 2
-TILE = NX * CHUNK
+PIECE = NX * CHUNK
+TILE = 2 * PIECE
+SUB = 128
 T_LOCAL = 14
 S_LOCAL = 7
 SCALE = 1.0 / math.sqrt(DH)
@@ -63,6 +66,7 @@
     sums_dp,
     group_table,
     student_table,
+    levels,
     local_sem,
     swap_send,
     swap_recv,
@@ -108,31 +112,48 @@
     fill_t.start()
     fill_q.start()
 
+    partner = device(dp, 1 - head, kv)
+    near = (
+        partner,
+        device(dp, head, right),
+        device(dp, head, left),
+        device(dp, head, (kv + NX) % N_KV),
+        device(dp, head, (kv + N_KV - NX) % N_KV),
+    )
     barrier = pltpu.get_barrier_semaphore()
 
-    def greet_plane(i, _):
-        peer = (head * N_KV + kv + i) % (2 * N_KV)
-        pl.semaphore_signal(
-            barrier,
-            inc=1,
-            device_id=device(dp, peer // N_KV, peer % N_KV),
-            device_id_type=MESH,
-        )
-        return 0
-
-    lax.fori_loop(1, 2 * N_KV, greet_plane, 0)
-
-    def greet_dp(i, _):
+    def greet_near(semaphore):
+        for peer in near:
+            pl.semaphore_signal(semaphore, inc=1, device_id=peer, device_id_type=MESH)
+
+    greet_near(barrier)
+    for i in range(1, N_DP):
         pl.semaphore_signal(
             barrier, inc=1, device_id=device((dp + i) % N_DP, head, kv), device_id_type=MESH
         )
-        return 0
-
-    lax.fori_loop(1, N_DP, greet_dp, 0)
-    pl.semaphore_wait(barrier, 2 * N_KV - 1 + N_DP - 1)
-
-    partner = device(dp, 1 - head, kv)
+
+    def columns(h):
+        return pl.ds(pl.multiple_of(h * DH, DH), DH)
+
+    fill_q.wait()
+
+    def prepare_student(t, _):
+        qs[t] = split_scaled(sq[head, :, columns(t)])
+        s_state[t] = jnp.concatenate(
+            [jnp.full((8, ROWS), NEG, jnp.float32), jnp.zeros((8, ROWS), jnp.float32)], axis=0
+        )
+        return 0
+
+    lax.fori_loop(0, S_LOCAL, prepare_student, 0)
+    bias_col = col * ROWS + lax.broadcasted_iota(jnp.int32, (PIECE, ROWS), 1)
+    bias_pos = lax.broadcasted_iota(jnp.int32, (PIECE, ROWS), 0)
+    bias_key = bias_pos + (bias_pos // CHUNK) * (ROWS - CHUNK)
+    for c in range(2):
+        bias[c * PIECE : (c + 1) * PIECE] = jnp.where(bias_key + c * CHUNK <= bias_col, 0.0, NEG)
     fill_s.wait()
+    fill_t.wait()
+    pl.semaphore_wait(barrier, len(near) + N_DP - 1)
+
     swap_s = remote(
         keys.at[kv, :, pl.ds(s_lane, 128)],
         keys.at[kv, :, pl.ds(s_lane, 128)],
@@ -141,19 +162,41 @@
         partner,
     )
     swap_s.start()
-    fill_q.wait()
+    greet_near(levels.at[0])
     swap_q = remote(sq.at[head], sq.at[head], swap_send.at[1], swap_recv.at[1], partner)
-
-    bias_col = col * ROWS + lax.broadcasted_iota(jnp.int32, (TILE, ROWS), 1)
-    bias_pos = lax.broadcasted_iota(jnp.int32, (TILE, ROWS), 0)
-    bias_key = bias_pos + (bias_pos // CHUNK) * (ROWS - CHUNK)
-    for c in range(2):
-        bias[c] = jnp.where(bias_key + c * CHUNK <= bias_col, 0.0, NEG)
-
-    def columns(h):
-        return pl.ds(pl.multiple_of(h * DH, DH), DH)
-
-    fill_t.wait()
+    last_row = row == NZ - 1
+
+    @pl.when(last_row)
+    def _():
+        swap_q.start()
+
+
+    def student_of(t):
+        found = jnp.int32(0)
+        for e in range(HT):
+            found = jnp.where(table[e // 2, e % 2] == head * T_LOCAL + t, e // 2, found)
+        return found
+
+    students = [student_of(t) for t in range(T_LOCAL)]
+    for t in range(T_LOCAL):
+        student_table[t] = students[t]
+        group_table[t] = jnp.where(students[t] >= GROUP, 1, 0)
+
+    def prepare(t, _):
+        q = tq[0, :, columns(t)]
+        qy[t] = split_scaled(q)
+        s = student_table[t]
+        minus_q = jnp.zeros((ROWS, DH), jnp.bfloat16)
+        for e in range(S_LOCAL):
+            candidate = -sq[head, :, e * DH : (e + 1) * DH]
+            minus_q = jnp.where(s == head * S_LOCAL + e, candidate, minus_q)
+        qg[t] = jnp.concatenate([q, minus_q], axis=1)
+        t_state[t] = jnp.concatenate(
+            [jnp.full((8, ROWS), NEG, jnp.float32), jnp.zeros((16, ROWS), jnp.float32)], axis=0
+        )
+        return 0
+
+    lax.fori_loop(0, T_LOCAL, prepare, 0)
     other_lane = pl.multiple_of(384 - head * 128, 128)
     landed_s = remote(
         keys.at[kv, :, pl.ds(other_lane, 128)],
@@ -177,10 +220,10 @@
         return z_copy(row, c, z_send.at[1, c], (row + NZ - 1) % NZ)
 
     has_up = row < NZ - 1
-    has_down = row < 2
+    has_down = (row == 0, row < 2)
 
     def forward(slot_row, c):
-        return z_copy(slot_row, c, relay_send.at[c], jnp.where(row == 0, NZ - 1, row + 1))
+        return z_copy(slot_row, c, relay_send.at[c], jnp.where(row == 0, NZ - 1, jnp.where(row == NZ - 1, 2, row + 1)))
 
     def x1(slot_row, c, side, target):
         block = keys.at[slot_row * NX + col, pl.ds(c * CHUNK, CHUNK)]
@@ -237,9 +280,9 @@
         z_copy(r, c, relay_send.at[c], row).wait_recv()
         start_x1(r, c)
 
-        @pl.when((row == 1) & (r == 0))
+        @pl.when(((row == NZ - 1) & (r == 0)) | ((row == 2) & (r == 1) & (c == 0)))
         def _():
-            forward(0, c).start()
+            forward(r, c).start()
 
     def x_event(w):
         r, c = wave(w)
@@ -253,157 +296,180 @@
         x2(r, c, 0, far_col, right).wait_recv()
         x2(r, c, 1, far_col, right).wait_recv()
 
-    for c in range(2):
-        start_x1(row, c)
-
+    def start_z(c):
         @pl.when(has_up)
         def _():
             up(c).start()
 
-        @pl.when(has_down)
+        @pl.when(has_down[c])
         def _():
             down(c).start()
 
-    swap_q.start()
-
-    def prepare(t, _):
-        qy[t] = split_scaled(tq[0, :, columns(t)])
-        t_state[t] = jnp.concatenate(
-            [jnp.full((8, ROWS), NEG, jnp.float32), jnp.zeros((16, ROWS), jnp.float32)], axis=0
-        )
-        return 0
-
-    lax.fori_loop(0, T_LOCAL, prepare, 0)
-
-    def prepare_student(t, _):
-        qs[t] = split_scaled(sq[head, :, columns(t)])
-        s_state[t] = jnp.concatenate(
-            [jnp.full((8, ROWS), NEG, jnp.float32), jnp.zeros((8, ROWS), jnp.float32)], axis=0
-        )
-        return 0
-
-    lax.fori_loop(0, S_LOCAL, prepare_student, 0)
+    for c in range(2):
+        start_x1(row, c)
+    start_z(0)
+
+    @pl.when(jnp.logical_not(last_row))
+    def _():
+        swap_q.start()
 
     waves = 2 * (row + 1)
+
+    def events(event, *indices):
+        for w in indices:
+
+            @pl.when(w < waves)
+            def _():
+                event(w)
+
+    def next_level(i):
+        pl.semaphore_wait(levels.at[i - 1], len(near))
+        greet_near(levels.at[i])
+
     x_event(0)
     x_event(1)
+    start_z(1)
+    next_level(1)
+
+    @pl.when(last_row)
+    def _():
+        events(z_event, 2, 3)
+
+    remote(sq.at[1 - head], sq.at[1 - head], swap_send.at[1], swap_recv.at[1], partner).wait_recv()
 
     @pl.when(row == 0)
     def _():
-        for c in range(2):
-            z_copy(1, c, relay_send.at[c], row).wait_recv()
-            forward(1, c).start()
-
-    @pl.when(row > 0)
-    def _():
-        z_event(2)
-        z_event(3)
-
-    def student_of(t):
-        found = jnp.int32(0)
-        for e in range(HT):
-            found = jnp.where(table[e] == head * T_LOCAL + t, e // 2, found)
-        return found
-
-    students = [student_of(t) for t in range(T_LOCAL)]
-    for t in range(T_LOCAL):
-        student_table[t] = students[t]
-        group_table[t] = jnp.where(students[t] >= GROUP, 1, 0)
-
-    remote(sq.at[1 - head], sq.at[1 - head], swap_send.at[1], swap_recv.at[1], partner).wait_recv()
-
-    def prepare_gap(t, _):
+        z_copy(1, 1, relay_send.at[1], row).wait_recv()
+        forward(1, 1).start()
+
+    def prepare_far(t, _):
         s = student_table[t]
-        student_q = sq[0, :, 0:DH]
-        for e in range(1, HS):
-            candidate = sq[e // GROUP, :, (e % GROUP) * DH : (e % GROUP + 1) * DH]
-            student_q = jnp.where(s == e, candidate, student_q)
-        qg[t] = jnp.concatenate([tq[0, :, columns(t)], -student_q], axis=1)
-        return 0
-
-    lax.fori_loop(0, T_LOCAL, prepare_gap, 0)
-
-    def compute(r, c, masked):
-        def tile(lanes):
-            return keys[pl.ds(r * NX, NX), pl.ds(c * CHUNK, CHUNK), lanes].reshape(TILE, 128)
-
-        def product(lhs, rhs):
-            return lax.dot_general(lhs, rhs, NT, preferred_element_type=jnp.float32)
-
-        def teacher_products(t, group, lane, y_buf, g_buf):
-            k = tile(pl.ds(lane, 128))
-            ks = jnp.where(group == 0, tile(pl.ds(256, 128)), tile(pl.ds(384, 128)))
-            y_buf[...] = product(jnp.concatenate([k, k], axis=1), qy[t])
-            g_buf[...] = product(jnp.concatenate([k, ks], axis=1), qg[t])
-
-        def student_products(t):
-            k = tile(pl.ds(s_lane, 128))
-            y_s[...] = product(jnp.concatenate([k, k], axis=1), qs[t])
-
-        def weights(y_buf, running_max):
-            y = y_buf[...]
-            if masked:
-                y = y + bias[c]
-            y = y.reshape(TILE // 8, 8, ROWS)
-            new_max = jnp.maximum(running_max, jnp.max(y, axis=0))
-            return new_max, jnp.exp2(running_max - new_max), jnp.exp2(y - new_max[None])
-
-        def teacher_update(t, y_buf, g_buf):
-            new_max, rescale, p = weights(y_buf, t_state[t, 0:8])
-            t_state[t, 0:8] = new_max
-            t_state[t, 8:16] = t_state[t, 8:16] * rescale + jnp.sum(p, axis=0)
-            t_state[t, 16:24] = t_state[t, 16:24] * rescale + jnp.sum(
-                p * g_buf[...].reshape(p.shape), axis=0
-            )
-
-        def student_update(t):
-            new_max, rescale, p = weights(y_s, s_state[t, 0:8])
-            s_state[t, 0:8] = new_max
-            s_state[t, 8:16] = s_state[t, 8:16] * rescale + jnp.sum(p, axis=0)
-
-        teacher_products(0, group_table[0], 0, y_a, g_a)
-
-        def step(j, _):
-            following = jnp.minimum(j + 1, GROUP - 1)
-            teacher_products(GROUP + j, group_table[GROUP + j], 128, y_b, g_b)
-            student_products(j)
-            teacher_update(j, y_a, g_a)
-            teacher_products(following, group_table[following], 0, y_a, g_a)
-            teacher_update(GROUP + j, y_b, g_b)
-            student_update(j)
-            return 0
-
-        lax.fori_loop(0, GROUP, step, 0)
-
-    for w in range(2):
-
-        @pl.when(w + 4 < waves)
+        minus_q = qg[t, :, DH : 2 * DH]
+        for e in range(S_LOCAL):
+            candidate = -sq[1 - head, :, e * DH : (e + 1) * DH]
+            minus_q = jnp.where(s == (1 - head) * S_LOCAL + e, candidate, minus_q)
+        qg[t, :, DH : 2 * DH] = minus_q
+        return 0
+
+    lax.fori_loop(0, T_LOCAL, prepare_far, 0)
+
+    def pieces_of(k):
+        return wave(2 * k), wave(2 * k + 1)
+
+    def tile(pieces, lane):
+        return jnp.concatenate(
+            [
+                keys[pl.ds(r * NX, NX), pl.ds(c * CHUNK, CHUNK), pl.ds(lane, 128)].reshape(
+                    PIECE, 128
+                )
+                for r, c in pieces
+            ],
+            axis=0,
+        )
+
+    def product(lhs, rhs):
+        return lax.dot_general(lhs, rhs, NT, preferred_element_type=jnp.float32)
+
+    def teacher_products(pieces, t, lane, y_buf, g_buf):
+        group = group_table[t]
+        k_t = tile(pieces, lane)
+        k_s = jnp.where(group == 0, tile(pieces, 256), tile(pieces, 384))
+        y_buf[...] = product(jnp.concatenate([k_t, k_t], axis=1), qy[t])
+        g_buf[...] = product(jnp.concatenate([k_t, k_s], axis=1), qg[t])
+
+    def student_products(pieces, t):
+        k_s = tile(pieces, s_lane)
+        y_s[...] = product(jnp.concatenate([k_s, k_s], axis=1), qs[t])
+
+    def weights(y_buf, part, running_max, masked):
+        y = y_buf[part]
+        if masked:
+            y = y + bias[part]
+        y = y.reshape(SUB // 8, 8, ROWS)
+        new_max = jnp.maximum(running_max, jnp.max(y, axis=0))
+        return new_max, jnp.exp2(running_max - new_max), jnp.exp2(y - new_max[None])
+
+    parts_of_tile = [pl.ds(n * SUB, SUB) for n in range(TILE // SUB)]
+
+    def teacher_update(t, y_buf, g_buf, masked):
+        m, total, cross = t_state[t, 0:8], t_state[t, 8:16], t_state[t, 16:24]
+        for part in parts_of_tile:
+            m, rescale, p = weights(y_buf, part, m, masked)
+            total = total * rescale + jnp.sum(p, axis=0)
+            cross = cross * rescale + jnp.sum(p * g_buf[part].reshape(p.shape), axis=0)
+        t_state[t, 0:8] = m
+        t_state[t, 8:16] = total
+        t_state[t, 16:24] = cross
+
+    def student_update(t, masked):
+        m, total = s_state[t, 0:8], s_state[t, 8:16]
+        for part in parts_of_tile:
+            m, rescale, p = weights(y_s, part, m, masked)
+            total = total * rescale + jnp.sum(p, axis=0)
+        s_state[t, 0:8] = m
+        s_state[t, 8:16] = total
+
+    def step(masked, now, after, j, _):
+        final = j == GROUP - 1
+        later = [
+            tuple(jnp.where(final, new, old) for old, new in zip(*pair)) for pair in zip(now, after)
+        ]
+        teacher_products(now, GROUP + j, 128, y_b, g_b)
+        student_products(now, j)
+        teacher_update(j, y_a, g_a, masked)
+        teacher_products(later, jnp.where(final, 0, j + 1), 0, y_a, g_a)
+        teacher_update(GROUP + j, y_b, g_b, masked)
+        student_update(j, masked)
+        return 0
+
+    d_event(0)
+    d_event(1)
+    teacher_products(pieces_of(0), 0, 0, y_a, g_a)
+
+    def stretch(masked, n, _):
+        k = n // 3
+        part = n % 3
+
+        if masked:
+
+            @pl.when((part == 1) & last_row)
+            def _():
+                events(x_event, 2, 3)
+                events(z_event, 4, 5)
+
+            @pl.when((part == 1) & jnp.logical_not(last_row))
+            def _():
+                events(z_event, 2, 3)
+
+            @pl.when((part == 2) & jnp.logical_not(last_row))
+            def _():
+                events(x_event, 2, 3)
+                events(z_event, 4, 5)
+
+        else:
+
+            @pl.when(part == 0)
+            def _():
+                events(x_event, 2 * k + 2, 2 * k + 3)
+                events(z_event, 2 * k + 4, 2 * k + 5)
+
+        @pl.when(part == 2)
         def _():
-            z_event(w + 4)
-
-        @pl.when(w + 2 < waves)
-        def _():
-            x_event(w + 2)
-
-        d_event(w)
-        compute(row, w, True)
-
-    def later(w, _):
-        @pl.when(w + 4 < waves)
-        def _():
-            z_event(w + 4)
-
-        @pl.when(w + 2 < waves)
-        def _():
-            x_event(w + 2)
-
-        d_event(w)
-        r, c = wave(w)
-        compute(r, c, False)
-        return 0
-
-    lax.fori_loop(2, waves, later, 0)
-
+            events(d_event, 2 * k + 2, 2 * k + 3)
+
+        lax.fori_loop(
+            3 * part,
+            jnp.minimum(3 * part + 3, GROUP),
+            functools.partial(step, masked, pieces_of(k), pieces_of(jnp.minimum(k + 1, row))),
+            0,
+        )
+        return 0
+
+    lax.fori_loop(0, 3, functools.partial(stretch, True), 0)
+    next_level(2)
+    lax.fori_loop(3, 3 * (row + 1), functools.partial(stretch, False), 0)
+
+    next_level(3)
     lane_row = lax.broadcasted_iota(jnp.int32, (8, ROWS), 0)
     parts = [jnp.zeros((8, ROWS), jnp.float32), jnp.zeros((8, ROWS), jnp.float32)]
     for t in range(T_LOCAL):
@@ -425,6 +491,7 @@
         home = home + jnp.where(lane_row == t, (top + jnp.log2(total)) * (2.0 * LN2), 0.0)
     for g in range(2):
         contrib[g] = parts[g] + jnp.where(head == g, home, 0.0)
+    pl.semaphore_wait(levels.at[3], len(near))
     kl_copy = remote(contrib.at[1 - head], kl_other, kl_sem.at[0], kl_sem.at[1], partner)
     kl_copy.start()
 
@@ -494,17 +561,21 @@
         def _():
             up(c).wait_send()
 
-        @pl.when(has_down)
+        @pl.when(has_down[c])
         def _():
             down(c).wait_send()
 
-        @pl.when(row == 0)
-        def _():
-            forward(1, c).wait_send()
-
-        @pl.when(row == 1)
+        @pl.when(row == NZ - 1)
         def _():
             forward(0, c).wait_send()
+
+    @pl.when(row == 0)
+    def _():
+        forward(1, 1).wait_send()
+
+    @pl.when(row == 2)
+    def _():
+        forward(1, 0).wait_send()
 
     def drain(w, _):
         r, c = wave(w)
@@ -551,13 +622,14 @@
             pltpu.VMEM((TILE, ROWS), f32),
             pltpu.VMEM((TILE, ROWS), f32),
             pltpu.VMEM((TILE, ROWS), f32),
-            pltpu.VMEM((2, TILE, ROWS), f32),
+            pltpu.VMEM((TILE, ROWS), f32),
             pltpu.VMEM((2, 8, ROWS), f32),
             pltpu.VMEM((8, ROWS), f32),
             pltpu.VMEM((2 * N_KV + 2, 8, 128), f32),
             pltpu.VMEM((N_DP + 1, 8, 128), f32),
             pltpu.SMEM((T_LOCAL,), jnp.int32),
             pltpu.SMEM((T_LOCAL,), jnp.int32),
+            pltpu.SemaphoreType.REGULAR((4,)),
             dma((3,)),
             dma((2,)),
             dma((2,)),
@@ -577,7 +649,7 @@
         compiler_params=pltpu.CompilerParams(
             collective_id=0, has_side_effects=True, vmem_limit_bytes=60 * 1024 * 1024
         ),
-    )(pair_table.reshape(-1), teacher_query, teacher_key, student_query, student_key)
+    )(pair_table, teacher_query, teacher_key, student_query, student_key)
     return kl, loss[:S_LOCAL, 0]
 
 

time: 95.3 us -> 87.4 us (0.917)
  Pallas kernels: 91.1 us -> 83.3 us
    pallas_call x1, Pallas kernels: 91.1 us -> 83.3 us  [per_device(): pl.pallas_call(kernel, out_shape=(jax.ShapeDtypeStruct((1, S_LOCAL, ROWS)...]
where the time goes in v2:
time: 87.4 us; the launch traced here: 87.2 us
  Pallas kernels  83.3 us (95%)
  local copies, waits for them, and re-layouts  3.28 us (4%)
    pallas_call x1, Pallas kernels, per_device(): pl.pallas_call(kernel, out_shape=(jax.ShapeDtypeStruct((1, S_LOCAL, ROWS)...  83.3 us
    unnamed x4, local copies, waits for them, and re-layouts  2.66 us

profile of v2, /device:TPU:1, one launch (start us, length us, event | category | flops | bytes accessed | tf_op | source)
XLA Modules:
  0.0 87.2 jit_solution(16922474541372024636)
XLA Ops:
  0.6 1.4 %copy.9.table = s32[14,2]{1,0:T(8,128)} copy(s32[14,2]{0,1:T(2,128)} %param.9) | data formatting | bytes 224 | tf_op args[4]
  2.0 83.3 %shard_map.68 = (f32[1,7,256]{2,1,0:T(8,128)}, f32[8,128]{1,0:T(8,128)}) custom-call(s32[14,2]{1,0:T(8,128)} %copy.9.table, bf16[1,256,1792]{2,1,0:T(8,128)(2,1)} %tq.1, bf16[1,256,256]{2,1,0:T(8,128)(2,1)} %tk_in.1, bf16[1,256,896]{2,1,0:T(8,128)(2,1)} %sq_in.1, bf16[1,256,128]{2,1,0:T(8,128)(2,1)} %sk_in.1), custom_call_target="tpu_custom_call" | custom-call | tf_op jit(solution)/shard_map/pallas_call | solution.py:604
  85.3 0.0 copy-start
  85.3 1.3 %copy.10 = f32[1,7,256]{2,0,1:T(1,128)} copy(f32[1,7,256]{2,1,0:T(8,128)} %get-tuple-element.8) | data formatting | bytes 14336
  86.6 0.0 copy-done
  86.6 0.6 slice_reduce_fusion
Async XLA Ops:
  85.3 1.3 %copy-start = (f32[8,128]{1,0:T(8,128)S(1)}, f32[8,128]{1,0:T(8,128)}, u32[]{:S(2)}) copy-start(f32[8,128]{1,0:T(8,128)} %get-tuple-element.5) | copy-start | bytes 12292

commit v3 on v2

--- a/solution.py
+++ b/solution.py
@@ -59,6 +59,7 @@
     y_b,
     g_b,
     y_s,
+    first_p,
     bias,
     contrib,
     kl_other,
@@ -77,6 +78,8 @@
     x1_recv,
     x2_send,
     x2_recv,
+    own_send,
+    own_recv,
     kl_sem,
     plane_send,
     plane_recv,
@@ -139,9 +142,6 @@
 
     def prepare_student(t, _):
         qs[t] = split_scaled(sq[head, :, columns(t)])
-        s_state[t] = jnp.concatenate(
-            [jnp.full((8, ROWS), NEG, jnp.float32), jnp.zeros((8, ROWS), jnp.float32)], axis=0
-        )
         return 0
 
     lax.fori_loop(0, S_LOCAL, prepare_student, 0)
@@ -154,6 +154,17 @@
     fill_t.wait()
     pl.semaphore_wait(barrier, len(near) + N_DP - 1)
 
+    def own_part(c, side, part, target):
+        block = keys.at[kv, pl.ds(c * CHUNK, CHUNK), pl.ds(256 * part, 256)]
+        return remote(
+            block, block, own_send.at[c, side, part], own_recv.at[c, side, part], device(dp, head, target)
+        )
+
+    def start_own(part):
+        for c in range(2):
+            own_part(c, 0, part, right).start()
+            own_part(c, 1, part, left).start()
+
     swap_s = remote(
         keys.at[kv, :, pl.ds(s_lane, 128)],
         keys.at[kv, :, pl.ds(s_lane, 128)],
@@ -162,6 +173,7 @@
         partner,
     )
     swap_s.start()
+    start_own(0)
     greet_near(levels.at[0])
     swap_q = remote(sq.at[head], sq.at[head], swap_send.at[1], swap_recv.at[1], partner)
     last_row = row == NZ - 1
@@ -191,9 +203,6 @@
             candidate = -sq[head, :, e * DH : (e + 1) * DH]
             minus_q = jnp.where(s == head * S_LOCAL + e, candidate, minus_q)
         qg[t] = jnp.concatenate([q, minus_q], axis=1)
-        t_state[t] = jnp.concatenate(
-            [jnp.full((8, ROWS), NEG, jnp.float32), jnp.zeros((16, ROWS), jnp.float32)], axis=0
-        )
         return 0
 
     lax.fori_loop(0, T_LOCAL, prepare, 0)
@@ -257,6 +266,17 @@
             device(dp, head, target),
         )
 
+    def own_arrival(c, side, source_col):
+        for part in range(2):
+            block = keys.at[row * NX + source_col, pl.ds(c * CHUNK, CHUNK), pl.ds(256 * part, 256)]
+            remote(
+                block,
+                block,
+                own_send.at[c, side, part],
+                own_recv.at[c, side, part],
+                device(dp, head, right),
+            ).wait_recv()
+
     left_col = (col + NX - 1) % NX
     right_col = (col + 1) % NX
     far_col = (col + 2) % NX
@@ -305,9 +325,9 @@
         def _():
             down(c).start()
 
-    for c in range(2):
-        start_x1(row, c)
+    start_own(1)
     start_z(0)
+    start_z(1)
 
     @pl.when(jnp.logical_not(last_row))
     def _():
@@ -325,33 +345,6 @@
     def next_level(i):
         pl.semaphore_wait(levels.at[i - 1], len(near))
         greet_near(levels.at[i])
-
-    x_event(0)
-    x_event(1)
-    start_z(1)
-    next_level(1)
-
-    @pl.when(last_row)
-    def _():
-        events(z_event, 2, 3)
-
-    remote(sq.at[1 - head], sq.at[1 - head], swap_send.at[1], swap_recv.at[1], partner).wait_recv()
-
-    @pl.when(row == 0)
-    def _():
-        z_copy(1, 1, relay_send.at[1], row).wait_recv()
-        forward(1, 1).start()
-
-    def prepare_far(t, _):
-        s = student_table[t]
-        minus_q = qg[t, :, DH : 2 * DH]
-        for e in range(S_LOCAL):
-            candidate = -sq[1 - head, :, e * DH : (e + 1) * DH]
-            minus_q = jnp.where(s == (1 - head) * S_LOCAL + e, candidate, minus_q)
-        qg[t, :, DH : 2 * DH] = minus_q
-        return 0
-
-    lax.fori_loop(0, T_LOCAL, prepare_far, 0)
 
     def pieces_of(k):
         return wave(2 * k), wave(2 * k + 1)
@@ -370,6 +363,111 @@
     def product(lhs, rhs):
         return lax.dot_general(lhs, rhs, NT, preferred_element_type=jnp.float32)
 
+    def logits(pieces, t, lane, y_buf):
+        k_t = tile(pieces, lane)
+        y_buf[...] = product(jnp.concatenate([k_t, k_t], axis=1), qy[t])
+
+    def student_products(pieces, t):
+        k_s = tile(pieces, s_lane)
+        y_s[...] = product(jnp.concatenate([k_s, k_s], axis=1), qs[t])
+
+    def gaps(pieces, t, lane, g_buf):
+        group = group_table[t]
+        k_t = tile(pieces, lane)
+        k_s = jnp.where(group == 0, tile(pieces, 256), tile(pieces, 384))
+        g_buf[...] = product(jnp.concatenate([k_t, k_s], axis=1), qg[t])
+
+    parts_of_tile = [pl.ds(n * SUB, SUB) for n in range(TILE // SUB)]
+
+    def first_weights(y_buf, p_buf):
+        def masked(part):
+            return (y_buf[part] + bias[part]).reshape(SUB // 8, 8, ROWS)
+
+        m = jnp.max(masked(parts_of_tile[0]), axis=0)
+        for part in parts_of_tile[1:]:
+            m = jnp.maximum(m, jnp.max(masked(part), axis=0))
+        total = jnp.zeros((8, ROWS), jnp.float32)
+        for part in parts_of_tile:
+            p = jnp.exp2(masked(part) - m[None])
+            total = total + jnp.sum(p, axis=0)
+            if p_buf is not None:
+                p_buf[part] = p.reshape(SUB, ROWS)
+        return m, total
+
+    def first_teacher(t, y_buf):
+        m, total = first_weights(y_buf, first_p.at[t])
+        t_state[t, 0:8] = m
+        t_state[t, 8:16] = total
+
+    def first_student(t):
+        m, total = first_weights(y_s, None)
+        s_state[t, 0:8] = m
+        s_state[t, 8:16] = total
+
+    def first_cross(t, g_buf):
+        cross = jnp.zeros((8, ROWS), jnp.float32)
+        for part in parts_of_tile:
+            term = first_p[t, part] * g_buf[part]
+            cross = cross + jnp.sum(term.reshape(SUB // 8, 8, ROWS), axis=0)
+        t_state[t, 16:24] = cross
+
+    own = pieces_of(0)
+
+    def first_step(j, _):
+        logits(own, GROUP + j, 128, y_b)
+        student_products(own, j)
+        first_teacher(j, y_a)
+        logits(own, jnp.minimum(j + 1, GROUP - 1), 0, y_a)
+        first_teacher(GROUP + j, y_b)
+        first_student(j)
+        return 0
+
+    def cross_step(j, _):
+        gaps(own, GROUP + j, 128, g_b)
+        first_cross(j, g_a)
+        gaps(own, j + 1, 0, g_a)
+        first_cross(GROUP + j, g_b)
+        return 0
+
+    for c in range(2):
+        own_arrival(c, 0, left_col)
+        x2(row, c, 0, left_col, right).start()
+        own_arrival(c, 1, right_col)
+        x2(row, c, 1, right_col, left).start()
+    next_level(1)
+    events(z_event, 2)
+
+    @pl.when(row == 0)
+    def _():
+        z_copy(1, 1, relay_send.at[1], row).wait_recv()
+        forward(1, 1).start()
+
+    events(z_event, 3)
+    d_event(0)
+    d_event(1)
+    logits(own, 0, 0, y_a)
+    lax.fori_loop(0, 4, first_step, 0)
+    events(x_event, 2)
+    lax.fori_loop(4, GROUP, first_step, 0)
+    remote(sq.at[1 - head], sq.at[1 - head], swap_send.at[1], swap_recv.at[1], partner).wait_recv()
+    events(x_event, 3)
+    next_level(2)
+
+    @pl.when(last_row)
+    def _():
+        events(z_event, 4, 5)
+
+    def prepare_far(t, _):
+        s = student_table[t]
+        minus_q = qg[t, :, DH : 2 * DH]
+        for e in range(S_LOCAL):
+            candidate = -sq[1 - head, :, e * DH : (e + 1) * DH]
+            minus_q = jnp.where(s == (1 - head) * S_LOCAL + e, candidate, minus_q)
+        qg[t, :, DH : 2 * DH] = minus_q
+        return 0
+
+    lax.fori_loop(0, T_LOCAL, prepare_far, 0)
+
     def teacher_products(pieces, t, lane, y_buf, g_buf):
         group = group_table[t]
         k_t = tile(pieces, lane)
@@ -377,99 +475,78 @@
         y_buf[...] = product(jnp.concatenate([k_t, k_t], axis=1), qy[t])
         g_buf[...] = product(jnp.concatenate([k_t, k_s], axis=1), qg[t])
 
-    def student_products(pieces, t):
-        k_s = tile(pieces, s_lane)
-        y_s[...] = product(jnp.concatenate([k_s, k_s], axis=1), qs[t])
-
-    def weights(y_buf, part, running_max, masked):
-        y = y_buf[part]
-        if masked:
-            y = y + bias[part]
-        y = y.reshape(SUB // 8, 8, ROWS)
+    def weights(y_buf, part, running_max):
+        y = y_buf[part].reshape(SUB // 8, 8, ROWS)
         new_max = jnp.maximum(running_max, jnp.max(y, axis=0))
         return new_max, jnp.exp2(running_max - new_max), jnp.exp2(y - new_max[None])
 
-    parts_of_tile = [pl.ds(n * SUB, SUB) for n in range(TILE // SUB)]
-
-    def teacher_update(t, y_buf, g_buf, masked):
+    def teacher_update(t, y_buf, g_buf):
         m, total, cross = t_state[t, 0:8], t_state[t, 8:16], t_state[t, 16:24]
         for part in parts_of_tile:
-            m, rescale, p = weights(y_buf, part, m, masked)
+            m, rescale, p = weights(y_buf, part, m)
             total = total * rescale + jnp.sum(p, axis=0)
             cross = cross * rescale + jnp.sum(p * g_buf[part].reshape(p.shape), axis=0)
         t_state[t, 0:8] = m
         t_state[t, 8:16] = total
         t_state[t, 16:24] = cross
 
-    def student_update(t, masked):
+    def student_update(t):
         m, total = s_state[t, 0:8], s_state[t, 8:16]
         for part in parts_of_tile:
-            m, rescale, p = weights(y_s, part, m, masked)
+            m, rescale, p = weights(y_s, part, m)
             total = total * rescale + jnp.sum(p, axis=0)
         s_state[t, 0:8] = m
         s_state[t, 8:16] = total
 
-    def step(masked, now, after, j, _):
+    def step(now, after, j, _):
         final = j == GROUP - 1
         later = [
             tuple(jnp.where(final, new, old) for old, new in zip(*pair)) for pair in zip(now, after)
         ]
         teacher_products(now, GROUP + j, 128, y_b, g_b)
         student_products(now, j)
-        teacher_update(j, y_a, g_a, masked)
+        teacher_update(j, y_a, g_a)
         teacher_products(later, jnp.where(final, 0, j + 1), 0, y_a, g_a)
-        teacher_update(GROUP + j, y_b, g_b, masked)
-        student_update(j, masked)
-        return 0
-
-    d_event(0)
-    d_event(1)
-    teacher_products(pieces_of(0), 0, 0, y_a, g_a)
-
-    def stretch(masked, n, _):
+        teacher_update(GROUP + j, y_b, g_b)
+        student_update(j)
+        return 0
+
+    gaps(own, 0, 0, g_a)
+    lax.fori_loop(0, GROUP - 1, cross_step, 0)
+    events(d_event, 2, 3)
+    gaps(own, T_LOCAL - 1, 128, g_b)
+    first_cross(GROUP - 1, g_a)
+    teacher_products(pieces_of(jnp.minimum(1, row)), 0, 0, y_a, g_a)
+    first_cross(T_LOCAL - 1, g_b)
+    next_level(3)
+
+    def stretch(n, _):
         k = n // 3
         part = n % 3
 
-        if masked:
-
-            @pl.when((part == 1) & last_row)
-            def _():
-                events(x_event, 2, 3)
-                events(z_event, 4, 5)
-
-            @pl.when((part == 1) & jnp.logical_not(last_row))
-            def _():
-                events(z_event, 2, 3)
-
-            @pl.when((part == 2) & jnp.logical_not(last_row))
-            def _():
-                events(x_event, 2, 3)
-                events(z_event, 4, 5)
-
-        else:
-
-            @pl.when(part == 0)
-            def _():
-                events(x_event, 2 * k + 2, 2 * k + 3)
-                events(z_event, 2 * k + 4, 2 * k + 5)
+        @pl.when((part == 0) & (k == 1) & jnp.logical_not(last_row))
+        def _():
+            events(z_event, 4, 5)
+
+        @pl.when(part == 1)
+        def _():
+            events(x_event, 2 * k + 2, 2 * k + 3)
+            events(z_event, 2 * k + 4, 2 * k + 5)
 
         @pl.when(part == 2)
         def _():
             events(d_event, 2 * k + 2, 2 * k + 3)
 
         lax.fori_loop(
-            3 * part,
-            jnp.minimum(3 * part + 3, GROUP),
-            functools.partial(step, masked, pieces_of(k), pieces_of(jnp.minimum(k + 1, row))),
+            jnp.where(part == 0, 0, jnp.where(part == 1, 2, 6)),
+            jnp.where(part == 0, 2, jnp.where(part == 1, 6, GROUP)),
+            functools.partial(step, pieces_of(k), pieces_of(jnp.minimum(k + 1, row))),
             0,
         )
         return 0
 
-    lax.fori_loop(0, 3, functools.partial(stretch, True), 0)
-    next_level(2)
-    lax.fori_loop(3, 3 * (row + 1), functools.partial(stretch, False), 0)
-
-    next_level(3)
+    lax.fori_loop(3, 3 * (row + 1), stretch, 0)
+
     lane_row = lax.broadcasted_iota(jnp.int32, (8, ROWS), 0)
     parts = [jnp.zeros((8, ROWS), jnp.float32), jnp.zeros((8, ROWS), jnp.float32)]
     for t in range(T_LOCAL):
@@ -577,10 +654,19 @@
     def _():
         forward(1, 0).wait_send()
 
+    for c in range(2):
+        for part in range(2):
+            own_part(c, 0, part, right).wait_send()
+            own_part(c, 1, part, left).wait_send()
+
     def drain(w, _):
         r, c = wave(w)
-        x1(r, c, 0, right).wait_send()
-        x1(r, c, 1, left).wait_send()
+
+        @pl.when(w > 1)
+        def _():
+            x1(r, c, 0, right).wait_send()
+            x1(r, c, 1, left).wait_send()
+
         x2(r, c, 0, left_col, right).wait_send()
         x2(r, c, 1, right_col, left).wait_send()
         return 0
@@ -622,6 +708,7 @@
             pltpu.VMEM((TILE, ROWS), f32),
             pltpu.VMEM((TILE, ROWS), f32),
             pltpu.VMEM((TILE, ROWS), f32),
+            pltpu.VMEM((T_LOCAL, TILE, ROWS), f32),
             pltpu.VMEM((TILE, ROWS), f32),
             pltpu.VMEM((2, 8, ROWS), f32),
             pltpu.VMEM((8, ROWS), f32),
@@ -640,6 +727,8 @@
             dma((NZ, 2, 2)),
             dma((NZ, 2, 2)),
             dma((NZ, 2, 2)),
+            dma((2, 2, 2)),
+            dma((2, 2, 2)),
             dma((2,)),
             dma((2 * N_KV,)),
             dma((2 * N_KV,)),

time: 87.4 us -> 79.3 us (0.907)
  Pallas kernels: 83.3 us -> 75.2 us
    pallas_call x1, Pallas kernels: 83.3 us -> 75.2 us  [per_device(): pl.pallas_call(kernel, out_shape=(jax.ShapeDtypeStruct((1, S_LOCAL, ROWS)...]
where the time goes in v3:
time: 79.3 us; the launch traced here: 79.1 us
  Pallas kernels  75.2 us (95%)
  local copies, waits for them, and re-layouts  3.28 us (4%)
    pallas_call x1, Pallas kernels, per_device(): pl.pallas_call(kernel, out_shape=(jax.ShapeDtypeStruct((1, S_LOCAL, ROWS)...  75.2 us
    unnamed x4, local copies, waits for them, and re-layouts  2.66 us

profile of v3, /device:TPU:1, one launch (start us, length us, event | category | flops | bytes accessed | tf_op | source)
XLA Modules:
  0.0 79.1 jit_solution(13189134334512370967)
XLA Ops:
  0.6 1.4 %copy.9.table = s32[14,2]{1,0:T(8,128)} copy(s32[14,2]{0,1:T(2,128)} %param.9) | data formatting | bytes 224 | tf_op args[4]
  2.0 75.2 %shard_map.68 = (f32[1,7,256]{2,1,0:T(8,128)}, f32[8,128]{1,0:T(8,128)}) custom-call(s32[14,2]{1,0:T(8,128)} %copy.9.table, bf16[1,256,1792]{2,1,0:T(8,128)(2,1)} %tq.1, bf16[1,256,256]{2,1,0:T(8,128)(2,1)} %tk_in.1, bf16[1,256,896]{2,1,0:T(8,128)(2,1)} %sq_in.1, bf16[1,256,128]{2,1,0:T(8,128)(2,1)} %sk_in.1), custom_call_target="tpu_custom_call" | custom-call | tf_op jit(solution)/shard_map/pallas_call | solution.py:690
  77.2 0.0 copy-start
  77.2 1.3 %copy.10 = f32[1,7,256]{2,0,1:T(1,128)} copy(f32[1,7,256]{2,1,0:T(8,128)} %get-tuple-element.8) | data formatting | bytes 14336
  78.5 0.0 copy-done
  78.5 0.6 slice_reduce_fusion
Async XLA Ops:
  77.2 1.3 %copy-start = (f32[8,128]{1,0:T(8,128)S(1)}, f32[8,128]{1,0:T(8,128)}, u32[]{:S(2)}) copy-start(f32[8,128]{1,0:T(8,128)} %get-tuple-element.5) | copy-start | bytes 12292

commit v4 on v3

--- a/solution.py
+++ b/solution.py
@@ -41,13 +41,14 @@
 
 def kernel(
     table,
-    tq,
+    tq_in,
     tk_in,
     sq_in,
     sk_in,
     kl_out,
     loss_out,
     keys,
+    tq,
     sq,
     qy,
     qg,
@@ -111,9 +112,11 @@
     fill_t = pltpu.make_async_copy(tk_in.at[0], keys.at[kv, :, pl.ds(0, 256)], local_sem.at[0])
     fill_s = pltpu.make_async_copy(sk_in.at[0], keys.at[kv, :, pl.ds(s_lane, 128)], local_sem.at[1])
     fill_q = pltpu.make_async_copy(sq_in.at[0], sq.at[head], local_sem.at[2])
+    fill_tq = pltpu.make_async_copy(tq_in.at[0], tq, local_sem.at[3])
     fill_s.start()
     fill_t.start()
     fill_q.start()
+    fill_tq.start()
 
     partner = device(dp, 1 - head, kv)
     near = (
@@ -186,7 +189,7 @@
     def student_of(t):
         found = jnp.int32(0)
         for e in range(HT):
-            found = jnp.where(table[e // 2, e % 2] == head * T_LOCAL + t, e // 2, found)
+            found = jnp.where(table[e % 2, e // 2] == head * T_LOCAL + t, e // 2, found)
         return found
 
     students = [student_of(t) for t in range(T_LOCAL)]
@@ -195,7 +198,7 @@
         group_table[t] = jnp.where(students[t] >= GROUP, 1, 0)
 
     def prepare(t, _):
-        q = tq[0, :, columns(t)]
+        q = tq[:, columns(t)]
         qy[t] = split_scaled(q)
         s = student_table[t]
         minus_q = jnp.zeros((ROWS, DH), jnp.bfloat16)
@@ -205,6 +208,7 @@
         qg[t] = jnp.concatenate([q, minus_q], axis=1)
         return 0
 
+    fill_tq.wait()
     lax.fori_loop(0, T_LOCAL, prepare, 0)
     other_lane = pl.multiple_of(384 - head * 128, 128)
     landed_s = remote(
@@ -446,16 +450,18 @@
     d_event(0)
     d_event(1)
     logits(own, 0, 0, y_a)
-    lax.fori_loop(0, 4, first_step, 0)
+    lax.fori_loop(0, 3, first_step, 0)
     events(x_event, 2)
-    lax.fori_loop(4, GROUP, first_step, 0)
-    remote(sq.at[1 - head], sq.at[1 - head], swap_send.at[1], swap_recv.at[1], partner).wait_recv()
+    lax.fori_loop(3, 5, first_step, 0)
     events(x_event, 3)
-    next_level(2)
 
     @pl.when(last_row)
     def _():
         events(z_event, 4, 5)
+
+    lax.fori_loop(5, GROUP, first_step, 0)
+    remote(sq.at[1 - head], sq.at[1 - head], swap_send.at[1], swap_recv.at[1], partner).wait_recv()
+    next_level(2)
 
     def prepare_far(t, _):
         s = student_table[t]
@@ -528,7 +534,7 @@
         def _():
             events(z_event, 4, 5)
 
-        @pl.when(part == 1)
+        @pl.when(part == jnp.where(last_row & (k == 1), 0, 1))
         def _():
             events(x_event, 2 * k + 2, 2 * k + 3)
             events(z_event, 2 * k + 4, 2 * k + 5)
@@ -594,7 +600,9 @@
     lax.fori_loop(1, 2 * N_KV, plane_start, 0)
 
     kl_copy.wait()
-    kl_out[0] = (contrib[head] + kl_other[...])[0:S_LOCAL]
+    kl_rows = contrib[head] + kl_other[...]
+    for t in range(S_LOCAL):
+        kl_out[t] = kl_rows[t : t + 1]
 
     def plane_wait(i, total):
         source = (me + i) % (2 * N_KV)
@@ -690,13 +698,14 @@
     kl, loss = pl.pallas_call(
         kernel,
         out_shape=(
-            jax.ShapeDtypeStruct((1, S_LOCAL, ROWS), f32),
+            jax.ShapeDtypeStruct((S_LOCAL, 1, ROWS), f32),
             jax.ShapeDtypeStruct((8, 128), f32),
         ),
-        in_specs=[pl.BlockSpec(memory_space=pltpu.SMEM), vmem, anywhere, anywhere, anywhere],
+        in_specs=[pl.BlockSpec(memory_space=pltpu.SMEM), anywhere, anywhere, anywhere, anywhere],
         out_specs=(vmem, vmem),
         scratch_shapes=[
             pltpu.VMEM((N_KV, ROWS, 512), bf16),
+            pltpu.VMEM((ROWS, T_LOCAL * DH), bf16),
             pltpu.VMEM((2, ROWS, S_LOCAL * DH), bf16),
             pltpu.VMEM((T_LOCAL, ROWS, 256), bf16),
             pltpu.VMEM((T_LOCAL, ROWS, 256), bf16),
@@ -717,7 +726,7 @@
             pltpu.SMEM((T_LOCAL,), jnp.int32),
             pltpu.SMEM((T_LOCAL,), jnp.int32),
             pltpu.SemaphoreType.REGULAR((4,)),
-            dma((3,)),
+            dma((4,)),
             dma((2,)),
             dma((2,)),
             dma((2, 2)),
@@ -738,8 +747,8 @@
         compiler_params=pltpu.CompilerParams(
             collective_id=0, has_side_effects=True, vmem_limit_bytes=60 * 1024 * 1024
         ),
-    )(pair_table, teacher_query, teacher_key, student_query, student_key)
-    return kl, loss[:S_LOCAL, 0]
+    )(pair_table.T, teacher_query, teacher_key, student_query, student_key)
+    return jnp.transpose(kl, (1, 0, 2)), loss[:S_LOCAL, 0]
 
 
 def solution(mesh):

time: 79.3 us -> 76.3 us (0.962)
  Pallas kernels: 75.2 us -> 73.6 us
  local copies, waits for them, and re-layouts: 3.28 us -> 1.9 us
    unnamed x4 -> x3, local copies, waits for them, and re-layouts: 2.66 us -> 0.6 us
    pallas_call x1, Pallas kernels: 75.2 us -> 73.6 us  [per_device(): pl.pallas_call(kernel, out_shape=(jax.ShapeDtypeStruct((S_LOCAL, 1, ROWS)...]
where the time goes in v4:
time: 76.3 us; the launch traced here: 76.1 us
  Pallas kernels  73.6 us (96%)
  local copies, waits for them, and re-layouts  1.9 us (2%)
    pallas_call x1, Pallas kernels, per_device(): pl.pallas_call(kernel, out_shape=(jax.ShapeDtypeStruct((S_LOCAL, 1, ROWS)...  73.6 us

profile of v4, /device:TPU:1, one launch (start us, length us, event | category | flops | bytes accessed | tf_op | source)
XLA Modules:
  0.0 76.1 jit_solution(7615130119894078915)
XLA Ops:
  0.6 73.6 %shard_map.68 = (f32[7,1,256]{2,1,0:T(1,128)}, f32[8,128]{1,0:T(8,128)}) custom-call(s32[2,14]{1,0:T(2,128)} %bitcast.3, bf16[1,256,1792]{2,1,0:T(8,128)(2,1)} %tq_in.1, bf16[1,256,256]{2,1,0:T(8,128)(2,1)} %tk_in.1, bf16[1,256,896]{2,1,0:T(8,128)(2,1)} %sq_in.1, bf16[1,256,128]{2,1,0:T(8,128)(2,1)} %sk_in.1), custom_call_target="tpu_custom_call" | custom-call | tf_op jit(solution)/shard_map/pallas_call | solution.py:698
  74.2 0.0 copy-start
  74.2 1.3 %slice_reduce_fusion = f32[7]{0:T(128)} fusion(f32[8,128]{1,0:T(8,128)} %get-tuple-element.5), kind=kLoop, calls=%fused_computation | loop fusion | bytes 56 | tf_op jit(solution)/shard_map/slice | solution.py:751
  75.5 0.0 copy-done
  75.6 0.6 copy.8
Async XLA Ops:
  74.2 1.3 %copy-start = (f32[7,1,256]{2,1,0:T(1,128)S(1)}, f32[7,1,256]{2,1,0:T(1,128)}, u32[]{:S(2)}) copy-start(f32[7,1,256]{2,1,0:T(1,128)} %get-tuple-element.4) | copy-start | bytes 21508

commit v5 on v4

--- a/solution.py
+++ b/solution.py
@@ -599,6 +599,49 @@
 
     lax.fori_loop(1, 2 * N_KV, plane_start, 0)
 
+    swap_s.wait_send()
+    swap_q.wait_send()
+    for c in range(2):
+
+        @pl.when(has_up)
+        def _():
+            up(c).wait_send()
+
+        @pl.when(has_down[c])
+        def _():
+            down(c).wait_send()
+
+        @pl.when(row == NZ - 1)
+        def _():
+            forward(0, c).wait_send()
+
+    @pl.when(row == 0)
+    def _():
+        forward(1, 1).wait_send()
+
+    @pl.when(row == 2)
+    def _():
+        forward(1, 0).wait_send()
+
+    for c in range(2):
+        for part in range(2):
+            own_part(c, 0, part, right).wait_send()
+            own_part(c, 1, part, left).wait_send()
+
+    def drain(w, _):
+        r, c = wave(w)
+
+        @pl.when(w > 1)
+        def _():
+            x1(r, c, 0, right).wait_send()
+            x1(r, c, 1, left).wait_send()
+
+        x2(r, c, 0, left_col, right).wait_send()
+        x2(r, c, 1, right_col, left).wait_send()
+        return 0
+
+    lax.fori_loop(0, waves, drain, 0)
+
     kl_copy.wait()
     kl_rows = contrib[head] + kl_other[...]
     for t in range(S_LOCAL):
@@ -629,6 +672,11 @@
 
     for i in range(1, N_DP):
         dp_copy(i).start()
+    def plane_drain(i, _):
+        plane_copy(i).wait_send()
+        return 0
+
+    lax.fori_loop(1, 2 * N_KV, plane_drain, 0)
     grand = plane_total
     for i in range(1, N_DP):
         source = (dp + i) % N_DP
@@ -636,56 +684,13 @@
             sums_dp.at[source], sums_dp.at[source], dp_send.at[i], dp_recv.at[source], partner
         ).wait_recv()
         grand = grand + sums_dp[source]
-    loss_out[...] = grand * (1.0 / (N_DP * N_KV * ROWS))
-
-    swap_s.wait_send()
-    swap_q.wait_send()
-    for c in range(2):
-
-        @pl.when(has_up)
-        def _():
-            up(c).wait_send()
-
-        @pl.when(has_down[c])
-        def _():
-            down(c).wait_send()
-
-        @pl.when(row == NZ - 1)
-        def _():
-            forward(0, c).wait_send()
-
-    @pl.when(row == 0)
-    def _():
-        forward(1, 1).wait_send()
-
-    @pl.when(row == 2)
-    def _():
-        forward(1, 0).wait_send()
-
-    for c in range(2):
-        for part in range(2):
-            own_part(c, 0, part, right).wait_send()
-            own_part(c, 1, part, left).wait_send()
-
-    def drain(w, _):
-        r, c = wave(w)
-
-        @pl.when(w > 1)
-        def _():
-            x1(r, c, 0, right).wait_send()
-            x1(r, c, 1, left).wait_send()
-
-        x2(r, c, 0, left_col, right).wait_send()
-        x2(r, c, 1, right_col, left).wait_send()
-        return 0
-
-    lax.fori_loop(0, waves, drain, 0)
-
-    def plane_drain(i, _):
-        plane_copy(i).wait_send()
-        return 0
-
-    lax.fori_loop(1, 2 * N_KV, plane_drain, 0)
+    diagonal = lax.broadcasted_iota(jnp.int32, (8, 128), 0) == lax.broadcasted_iota(
+        jnp.int32, (8, 128), 1
+    )
+    loss_out[...] = jnp.sum(jnp.where(diagonal, grand, 0.0), axis=0, keepdims=True) * (
+        1.0 / (N_DP * N_KV * ROWS)
+    )
+
     for i in range(1, N_DP):
         dp_copy(i).wait_send()
 
@@ -699,7 +704,7 @@
         kernel,
         out_shape=(
             jax.ShapeDtypeStruct((S_LOCAL, 1, ROWS), f32),
-            jax.ShapeDtypeStruct((8, 128), f32),
+            jax.ShapeDtypeStruct((1, 128), f32),
         ),
         in_specs=[pl.BlockSpec(memory_space=pltpu.SMEM), anywhere, anywhere, anywhere, anywhere],
         out_specs=(vmem, vmem),
@@ -748,7 +753,7 @@
             collective_id=0, has_side_effects=True, vmem_limit_bytes=60 * 1024 * 1024
         ),
     )(pair_table.T, teacher_query, teacher_key, student_query, student_key)
-    return jnp.transpose(kl, (1, 0, 2)), loss[:S_LOCAL, 0]
+    return jnp.transpose(kl, (1, 0, 2)), loss[0, :S_LOCAL]
 
 
 def solution(mesh):

time: 76.3 us -> 75.9 us (level)
    slice x1 -> x0, local copies, waits for them, and re-layouts: 1.3 us -> none  [per_device(): return (jnp.transpose(kl, (1, 0, 2)), loss[:S_LOCAL, 0])]
    squeeze x0 -> x1, local copies, waits for them, and re-layouts: none -> 1.18 us  [per_device(): return (jnp.transpose(kl, (1, 0, 2)), loss[0, :S_LOCAL])]
where the time goes in v5:
time: 75.9 us; the launch traced here: 75.7 us
  Pallas kernels  73.3 us (97%)
  local copies, waits for them, and re-layouts  1.78 us (2%)
    pallas_call x1, Pallas kernels, per_device(): pl.pallas_call(kernel, out_shape=(jax.ShapeDtypeStruct((S_LOCAL, 1, ROWS)...  73.3 us

profile of v5, /device:TPU:1, one launch (start us, length us, event | category | flops | bytes accessed | tf_op | source)
XLA Modules:
  0.0 75.7 jit_solution(6293133027712108252)
XLA Ops:
  0.6 73.3 %shard_map.68 = (f32[7,1,256]{2,1,0:T(1,128)}, f32[1,128]{1,0:T(1,128)}) custom-call(s32[2,14]{1,0:T(2,128)} %bitcast.5, bf16[1,256,1792]{2,1,0:T(8,128)(2,1)} %tq_in.1, bf16[1,256,256]{2,1,0:T(8,128)(2,1)} %tk_in.1, bf16[1,256,896]{2,1,0:T(8,128)(2,1)} %sq_in.1, bf16[1,256,128]{2,1,0:T(8,128)(2,1)} %sk_in.1), custom_call_target="tpu_custom_call" | custom-call | tf_op jit(solution)/shard_map/pallas_call | solution.py:703
  73.9 0.0 copy-start
  73.9 1.2 %slice_bitcast_fusion = f32[7]{0:T(128)} fusion(f32[1,128]{1,0:T(1,128)} %get-tuple-element.5), kind=kLoop, calls=%fused_computation | loop fusion | bytes 56 | tf_op jit(solution)/shard_map/squeeze | solution.py:756
  75.1 0.0 copy-done
  75.1 0.6 copy.8
Async XLA Ops:
  73.9 1.2 %copy-start = (f32[7,1,256]{2,1,0:T(1,128)S(1)}, f32[7,1,256]{2,1,0:T(1,128)}, u32[]{:S(2)}) copy-start(f32[7,1,256]{2,1,0:T(1,128)} %get-tuple-element.4) | copy-start | bytes 21508

commit v6 on v5

--- a/solution.py
+++ b/solution.py
@@ -510,10 +510,10 @@
             tuple(jnp.where(final, new, old) for old, new in zip(*pair)) for pair in zip(now, after)
         ]
         teacher_products(now, GROUP + j, 128, y_b, g_b)
+        teacher_update(j, y_a, g_a)
         student_products(now, j)
-        teacher_update(j, y_a, g_a)
+        teacher_update(GROUP + j, y_b, g_b)
         teacher_products(later, jnp.where(final, 0, j + 1), 0, y_a, g_a)
-        teacher_update(GROUP + j, y_b, g_b)
         student_update(j)
         return 0
 

time: 75.9 us -> 75.9 us (level)
  no operation moved by 1% of the time
where the time goes in v6:
time: 75.9 us; the launch traced here: 75.7 us
  Pallas kernels  73.3 us (97%)
  local copies, waits for them, and re-layouts  1.78 us (2%)
    pallas_call x1, Pallas kernels, per_device(): pl.pallas_call(kernel, out_shape=(jax.ShapeDtypeStruct((S_LOCAL, 1, ROWS)...  73.3 us

profile of v6, /device:TPU:1, one launch (start us, length us, event | category | flops | bytes accessed | tf_op | source)
XLA Modules:
  0.0 75.7 jit_solution(6293133027712108252)
XLA Ops:
  0.6 73.3 %shard_map.68 = (f32[7,1,256]{2,1,0:T(1,128)}, f32[1,128]{1,0:T(1,128)}) custom-call(s32[2,14]{1,0:T(2,128)} %bitcast.5, bf16[1,256,1792]{2,1,0:T(8,128)(2,1)} %tq_in.1, bf16[1,256,256]{2,1,0:T(8,128)(2,1)} %tk_in.1, bf16[1,256,896]{2,1,0:T(8,128)(2,1)} %sq_in.1, bf16[1,256,128]{2,1,0:T(8,128)(2,1)} %sk_in.1), custom_call_target="tpu_custom_call" | custom-call | tf_op jit(solution)/shard_map/pallas_call | solution.py:703
  73.9 0.0 copy-start
  73.9 1.2 %slice_bitcast_fusion = f32[7]{0:T(128)} fusion(f32[1,128]{1,0:T(1,128)} %get-tuple-element.5), kind=kLoop, calls=%fused_computation | loop fusion | bytes 56 | tf_op jit(solution)/shard_map/squeeze | solution.py:756
  75.1 0.0 copy-done
  75.1 0.6 copy.8
Async XLA Ops:
  73.9 1.2 %copy-start = (f32[7,1,256]{2,1,0:T(1,128)S(1)}, f32[7,1,256]{2,1,0:T(1,128)}, u32[]{:S(2)}) copy-start(f32[7,1,256]{2,1,0:T(1,128)} %get-tuple-element.4) | copy-start | bytes 21508
